TPU v7x, 8 devices: a whole 2x2x1 slice. The times are simulated.
8 devices in a mesh: part: 1 (over z), tpa: 2 (over y), tpb: 4 (over x, core).
Axes of the slice: x: 2, y: 2, z: 1, core: 2. Of those that a mesh axis runs over, the one named last changes fastest.
Arguments:
- x: bfloat16 [64, 512, 2048], P(('part', 'tpb'))
- lengths: int32 [64], P(('part', 'tpb'))
- k_buf: bfloat16 [64, 512, 32, 64], P(('part', 'tpb'), None, 'tpa')
- v_buf: bfloat16 [64, 512, 32, 64], P(('part', 'tpb'), None, 'tpa')
- w_qkv: bfloat16 [2048, 6144], P('part', ('tpa', 'tpb'))
- w_o: bfloat16 [2048, 2048], P(('part', 'tpa', 'tpb'))
- w_gate_up: bfloat16 [2048, 16384], P('part', ('tpa', 'tpb'))
- w_down: bfloat16 [8192, 2048], P(('part', 'tpa', 'tpb'))
- g_attn: bfloat16 [2048], P('part')
- g_mlp: bfloat16 [2048], P('part')
Outputs:
- output 1: bfloat16 [64, 512, 2048], P(('part', 'tpb'))
- output 2: bfloat16 [64, 512, 32, 64], P(('part', 'tpb'), None, 'tpa')
- output 3: bfloat16 [64, 512, 32, 64], P(('part', 'tpb'), None, 'tpa')
- output 4: bfloat16 [2048, 2048], P('part', 'tpa')
- output 5: bfloat16 [2048, 2048], P('part', 'tpa')
- output 6: bfloat16 [2048, 2048], P('part', 'tpa')
- output 7: bfloat16 [2048, 2048], P(('part', 'tpa'))
- output 8: bfloat16 [2048, 8192], P('part', 'tpa')
- output 9: bfloat16 [2048, 8192], P('part', 'tpa')
- output 10: bfloat16 [8192, 2048], P(('part', 'tpa'))
All inputs are finite; a program needn't handle non-finite values.
Results may differ from a plain program's by a relative error of at most 0.0129807.
Values are sent between devices in bfloat16 or wider.
A program may use at most 1 GiB of HBM per device.

v0:
```python
import math
import jax
import jax.numpy as jnp
from jax import lax
from jax.sharding import PartitionSpec as P

ROPE_BASE = 500000.0
ROPE_FACTOR = 8.0
LOW_FREQ = 1.0
HIGH_FREQ = 4.0
ORIG_CONTEXT = 8192.0
NORM_EPS = 1e-5
MASK_VALUE = -1e30


def rms_norm(x_in, gain_vec):
    x_wide = x_in.astype(jnp.float32)
    mean_sq = jnp.mean(x_wide * x_wide, axis=-1, keepdims=True)
    return (x_wide * lax.rsqrt(mean_sq + NORM_EPS) * gain_vec.astype(jnp.float32)).astype(jnp.bfloat16)


def rope_tables(seq_len, head_dim):
    exponent = jnp.arange(head_dim // 2, dtype=jnp.float32) * (2.0 / head_dim)
    inv_freq = 1.0 / jnp.power(ROPE_BASE, exponent)
    wavelen = 2.0 * math.pi / inv_freq
    smooth = (ORIG_CONTEXT / wavelen - LOW_FREQ) / (HIGH_FREQ - LOW_FREQ)
    blended = (1.0 - smooth) * inv_freq / ROPE_FACTOR + smooth * inv_freq
    rope_freq = jnp.where(wavelen < ORIG_CONTEXT / HIGH_FREQ, inv_freq, jnp.where(wavelen > ORIG_CONTEXT / LOW_FREQ, inv_freq / ROPE_FACTOR, blended))
    angles = jnp.arange(seq_len, dtype=jnp.float32)[:, None] * rope_freq[None, :]
    return jnp.cos(angles), jnp.sin(angles)


def apply_rope(vec_in, cos_tab, sin_tab):
    half_dim = vec_in.shape[-1] // 2
    first_half = vec_in[..., :half_dim]
    second_half = vec_in[..., half_dim:]
    return jnp.concatenate([first_half * cos_tab - second_half * sin_tab, second_half * cos_tab + first_half * sin_tab], axis=-1)


def split_weights(qkv_cols, gu_cols, kv_local, head_dim, n_tpb):
    model_dim = qkv_cols.shape[0]
    group_size = qkv_cols.shape[1] // (kv_local * head_dim) - 2
    packed = qkv_cols.reshape(model_dim, kv_local, group_size + 2, head_dim)
    w_query = packed[:, :, :group_size, :].reshape(model_dim, kv_local * group_size * head_dim)
    w_key = packed[:, :, group_size, :].reshape(model_dim, kv_local * head_dim)
    w_value = packed[:, :, group_size + 1, :].reshape(model_dim, kv_local * head_dim)
    ff_block = gu_cols.shape[1] // (2 * n_tpb)
    gu_view = gu_cols.reshape(model_dim, n_tpb, 2, ff_block)
    w_gate = gu_view[:, :, 0, :].reshape(model_dim, n_tpb * ff_block)
    w_up = gu_view[:, :, 1, :].reshape(model_dim, n_tpb * ff_block)
    return w_query, w_key, w_value, w_gate, w_up


def prefill(x_loc, len_loc, k_buf, v_buf, qkv_cols, o_rows, gu_cols, down_rows, g_attn, g_mlp, n_tpb):
    batch_loc, seq_len, model_dim = x_loc.shape
    kv_local = k_buf.shape[2]
    head_dim = k_buf.shape[3]
    group_size = qkv_cols.shape[1] // (kv_local * head_dim) - 2
    x_normed = rms_norm(x_loc, g_attn)
    qkv_act = jnp.einsum('bsd,dc->bsc', x_normed, qkv_cols, preferred_element_type=jnp.float32).astype(jnp.bfloat16)
    qkv_act = qkv_act.reshape(batch_loc, seq_len, kv_local, group_size + 2, head_dim)
    cos_tab, sin_tab = rope_tables(seq_len, head_dim)
    q_rot = apply_rope(qkv_act[:, :, :, :group_size, :].astype(jnp.float32), cos_tab[:, None, None, :], sin_tab[:, None, None, :]).astype(jnp.bfloat16)
    k_rot = apply_rope(qkv_act[:, :, :, group_size, :].astype(jnp.float32), cos_tab[:, None, :], sin_tab[:, None, :]).astype(jnp.bfloat16)
    values = qkv_act[:, :, :, group_size + 1, :]
    scores = jnp.einsum('bqkgd,bskd->bkgqs', q_rot, k_rot, preferred_element_type=jnp.float32) * head_dim ** -0.5
    positions = jnp.arange(seq_len)
    allowed = (positions[None, None, :] <= positions[None, :, None]) & (positions[None, None, :] < len_loc[:, None, None])
    scores = jnp.where(allowed[:, None, None], scores, MASK_VALUE)
    attn_prob = jax.nn.softmax(scores, axis=-1).astype(jnp.bfloat16)
    attn_out = jnp.einsum('bkgqs,bskd->bqkgd', attn_prob, values, preferred_element_type=jnp.float32).astype(jnp.bfloat16)
    attn_out = attn_out.reshape(batch_loc, seq_len, kv_local * group_size * head_dim)
    attn_part = jnp.einsum('bsh,hd->bsd', attn_out, o_rows, preferred_element_type=jnp.float32).astype(jnp.bfloat16)
    attn_sum = lax.psum(attn_part, 'tpa')
    hidden = (x_loc.astype(jnp.float32) + attn_sum.astype(jnp.float32)).astype(jnp.bfloat16)
    h_normed = rms_norm(hidden, g_mlp)
    ff_block = gu_cols.shape[1] // (2 * n_tpb)
    gu_act = jnp.einsum('bsd,dc->bsc', h_normed, gu_cols, preferred_element_type=jnp.float32).astype(jnp.bfloat16)
    gu_act = gu_act.reshape(batch_loc, seq_len, n_tpb, 2, ff_block)
    mid_act = (jax.nn.silu(gu_act[..., 0, :].astype(jnp.float32)) * gu_act[..., 1, :].astype(jnp.float32)).astype(jnp.bfloat16)
    mid_act = mid_act.reshape(batch_loc, seq_len, n_tpb * ff_block)
    mlp_part = jnp.einsum('bsf,fd->bsd', mid_act, down_rows, preferred_element_type=jnp.float32).astype(jnp.bfloat16)
    mlp_sum = lax.psum(mlp_part, 'tpa')
    layer_out = (hidden.astype(jnp.float32) + mlp_sum.astype(jnp.float32)).astype(jnp.bfloat16)
    valid_pos = (positions[None, :] < len_loc[:, None])[:, :, None, None]
    k_cache = jnp.where(valid_pos, k_rot, k_buf)
    v_cache = jnp.where(valid_pos, values, v_buf)
    return layer_out, k_cache, v_cache


def solution(mesh):
    n_tpb = mesh.shape['tpb']

    def local_step(x_loc, len_loc, k_buf, v_buf, w_qkv, w_o, w_gate_up, w_down, g_attn, g_mlp):
        qkv_cols = lax.all_gather(w_qkv, 'tpb', axis=1, tiled=True)
        o_rows = lax.all_gather(w_o, 'tpb', axis=0, tiled=True)
        gu_cols = lax.all_gather(w_gate_up, 'tpb', axis=1, tiled=True)
        down_rows = lax.all_gather(w_down, 'tpb', axis=0, tiled=True)
        w_query, w_key, w_value, w_gate, w_up = split_weights(qkv_cols, gu_cols, k_buf.shape[2], k_buf.shape[3], n_tpb)
        layer_out, k_cache, v_cache = prefill(x_loc, len_loc, k_buf, v_buf, qkv_cols, o_rows, gu_cols, down_rows, g_attn, g_mlp, n_tpb)
        return (layer_out, k_cache, v_cache, w_query, w_key, w_value, o_rows, w_gate, w_up, down_rows)

    batch_spec = P(('part', 'tpb'), None, None)
    len_spec = P(('part', 'tpb'))
    cache_spec = P(('part', 'tpb'), None, 'tpa', None)
    train_cols = P('part', ('tpa', 'tpb'))
    train_rows = P(('part', 'tpa', 'tpb'), None)
    gain_spec = P('part')
    gen_cols = P('part', 'tpa')
    gen_rows = P(('part', 'tpa'), None)
    return jax.shard_map(local_step, mesh=mesh, in_specs=(batch_spec, len_spec, cache_spec, cache_spec, train_cols, train_rows, train_cols, train_rows, gain_spec, gain_spec), out_specs=(batch_spec, cache_spec, cache_spec, gen_cols, gen_cols, gen_cols, gen_rows, gen_cols, gen_cols, gen_rows), check_vma=False)
```

profile of v0, /device:TPU:0, one launch (start us, length us, event | category | flops | bytes accessed | tf_op | source)
XLA Modules:
  0.0 4287.9 jit_solution(14576019143319836296)
XLA Ops:
  7.2 0.0 all-gather.5.cloned.1.call-start
  7.2 0.7 all-gather.5.cloned.1.call-update
  7.9 0.0 all-gather.7.cloned.1.call-start
  8.0 0.7 all-gather.7.cloned.1.call-update
  8.7 0.0 all-reduce.3.cloned.1.call-start
  8.7 0.1 iota_compare_fusion
  8.8 0.7 iota_compare_fusion.1
  9.5 0.0 copy-start.2
  9.6 0.7 convert_element_type.89
  10.2 11.3 fusion.6
  21.6 1.0 fusion.42
  22.6 0.0 copy-done.2
  22.6 3.6 broadcast_and_fusion
  26.1 66.2 %all-gather.5.cloned.1.call-done = bf16[2048,3072]{1,0:T(8,128)(2,1)} async-done(((bf16[2048,768]{1,0:T(8,128)(2,1)}), bf16[2048,3072]{1,0:T(8,128)(2,1)}) %all-gather.5.cloned.1.call-update) | async-done | bytes 12582928 | tf_op jit(solution)/shard_map/all_gather | solution.py:95
  92.3 114.3 %fusion.23 = bf16[16,512,3072]{2,1,0:T(8,128)(2,1)} fusion(bf16[16,512,2048]{2,1,0:T(8,128)(2,1)} %param.10, f32[2048]{0:T(1024)S(1)} %convert_element_type.89, f32[16,512]{1,0:T(8,128)S(1)} %add_rsqrt_fusion.1, bf16[2048,3072]{1,0:T(8,128)(2,1)} %all-gather.5.cloned.1.call-done), kind=kOutput, calls=%fused_computation.34 | convolution fusion | flops 103171489792 | bytes 96509952 | tf_op jit(solution)/shard_map/bsd,dc->bsc/dot_general | solution.py:60
  206.6 59.3 %copy.25 = bf16[16,512,3072]{1,2,0:T(8,128)(2,1)} copy(bf16[16,512,3072]{2,1,0:T(8,128)(2,1)} %fusion.23) | data formatting | bytes 100663296 | tf_op jit(solution)/shard_map/convert_element_type | solution.py:60
  265.9 0.0 copy-start
  265.9 34.0 fusion.28
  299.9 0.0 copy-done
  299.9 0.0 copy-done.1
  299.9 17.6 subtract_convert_fusion.1
  317.5 17.3 fusion.38
  334.8 101.5 %fusion.1 = (f32[16,16,512]{2,1,0:T(8,128)S(1)}, f32[16,16,512,512]{3,2,1,0:T(8,128)}) fusion(pred[16,512,512]{1,2,0:T(8,128)(4,1)} %broadcast_and_fusion, bf16[16,512,16,32]{1,3,2,0:T(8,128)(2,1)} %get-tuple-element.27, bf16[16,512,16,32]{1,3,2,0:T(8,128)(2,1)} %get-tuple-element.26, bf16[16,512,16,32]{1,3,2,0:T(8,128)(2,1)} %get-tuple-element.25, ...), kind=kOutput, calls=%fused_computation.4 | convolution fusion | flops 8858238976 | bytes 306708480 | tf_op jit(solution)/shard_map/bqkgd,bskd->bkgqs/dot_general | solution.py:66
  436.2 82.0 %fusion = f32[16,16,512]{2,1,0:T(8,128)S(1)} fusion(f32[16,16,512,512]{3,2,1,0:T(8,128)} %get-tuple-element.38, f32[16,16,512]{2,1,0:T(8,128)S(1)} %get-tuple-element.37, pred[16,512,512]{1,2,0:T(8,128)(4,1)} %broadcast_and_fusion), kind=kLoop, calls=%fused_computation.3 | loop fusion | flops 268304384 | bytes 273678336 | tf_op jit(solution)/shard_map/reduce_sum | solution.py:70
  518.2 103.9 %fusion.35 = bf16[16,16,64,512]{3,2,1,0:T(8,128)(2,1)} fusion(f32[16,16,512]{2,1,0:T(8,128)S(1)} %fusion, f32[16,16,512]{2,1,0:T(8,128)S(1)} %get-tuple-element.37, f32[16,16,512,512]{3,2,1,0:T(8,128)} %get-tuple-element.38, pred[16,512,512]{1,2,0:T(8,128)(4,1)} %broadcast_and_fusion, bf16[16,512,16,3,64]{1,4,3,2,0:T(8,128)(2,1)} %bitcast.79), kind=kOutput, calls=%fused_computation.55 | convolution fusion | flops 8933867520 | bytes 307232768 | tf_op jit(solution)/shard_map/bkgqs,bskd->bqkgd/dot_general | solution.py:71
  622.1 0.0 all-gather.7.cloned.1.call-done
  622.1 45.7 %convolution_convert_fusion.1 = bf16[16,512,2048]{2,1,0:T(8,128)(2,1)} fusion(bf16[16,512,1024]{1,2,0:T(8,128)(2,1)} %bitcast.87, bf16[1024,2048]{1,0:T(8,128)(2,1)} %all-gather.7.cloned.1.call-done), kind=kOutput, calls=%fused_computation.36 | convolution fusion | flops 34376515584 | bytes 54525952 | tf_op jit(solution)/shard_map/bsh,hd->bsd/dot_general | solution.py:73
  667.8 0.0 copy-start.4
  667.8 0.0 all-reduce.3.cloned.1.call-update
  667.9 0.0 all-gather.9.cloned.1.call-start
  667.9 0.5 all-gather.9.cloned.1.call-update
  668.4 0.0 all-gather.11.cloned.1.call-start
  668.5 0.5 all-gather.11.cloned.1.call-update
  669.0 0.0 all-reduce.5.cloned.1.call-start
  669.1 0.0 copy-done.4
  669.1 730.7 %all-reduce.3.cloned.1.call-done = bf16[16,512,2048]{2,1,0:T(8,128)(2,1)} async-done(((bf16[16,512,2048]{2,1,0:T(8,128)(2,1)}), bf16[16,512,2048]{2,1,0:T(8,128)(2,1)}) %all-reduce.3.cloned.1.call-update) | async-done | bytes 33554448 | tf_op jit(solution)/shard_map/psum | solution.py:74
  1399.8 21.3 fusion.10
  1421.2 180.8 %all-gather.9.cloned.1.call-done = bf16[2048,8192]{1,0:T(8,128)(2,1)} async-done(((bf16[2048,2048]{1,0:T(8,128)(2,1)}), bf16[2048,8192]{1,0:T(8,128)(2,1)}) %all-gather.9.cloned.1.call-update) | async-done | bytes 33554448 | tf_op jit(solution)/shard_map/all_gather | solution.py:97
  1602.0 293.1 %convolution_convert_fusion = bf16[16,512,8192]{2,1,0:T(8,128)(2,1)} fusion(bf16[2048,8192]{1,0:T(8,128)(2,1)} %all-gather.9.cloned.1.call-done, f32[2048]{0:T(1024)S(1)} %convert_element_type.103, f32[16,512]{1,0:T(8,128)S(1)} %add_rsqrt_fusion, bf16[16,512,2048]{2,1,0:T(8,128)(2,1)} %param.10, bf16[16,512,2048]{2,1,0:T(8,128)(2,1)} %all-reduce.3.cloned.1.call-done), kind=kOutput, calls=%fused_computation.18 | convolution fusion | flops 275079233536 | bytes 234921984 | tf_op jit(solution)/shard_map/bsd,dc->bsc/dot_general | solution.py:78
  1895.1 213.2 %reshape.266 = bf16[16,512,4,2,1024]{4,3,2,1,0:T(2,128)(2,1)} reshape(bf16[16,512,8192]{2,1,0:T(8,128)(2,1)} %convolution_convert_fusion) | data formatting | bytes 268435456 | tf_op jit(solution)/shard_map/reshape | solution.py:79
  2108.3 908.3 %fusion.3 = (f32[16,512,4,1024]{3,2,1,0:T(4,128)}, f32[16,512,4,1024]{3,2,1,0:T(4,128)}) fusion(bf16[16,512,4,2,1024]{4,3,2,1,0:T(2,128)(2,1)} %reshape.266), kind=kLoop, calls=%fused_computation.8 | loop fusion | flops 67108864 | bytes 402653184 | tf_op jit(solution)/shard_map/convert_element_type | solution.py:80
  3016.5 155.2 %reshape.271 = f32[16,512,4096]{2,1,0:T(8,128)} reshape(f32[16,512,4,1024]{3,2,1,0:T(4,128)} %get-tuple-element.20) | data formatting | bytes 268435456 | tf_op jit(solution)/shard_map/convert_element_type | solution.py:80
  3171.8 155.2 %reshape.272 = f32[16,512,4096]{2,1,0:T(8,128)} reshape(f32[16,512,4,1024]{3,2,1,0:T(4,128)} %get-tuple-element.21) | data formatting | bytes 268435456 | tf_op jit(solution)/shard_map/convert_element_type | solution.py:80
  3327.0 0.0 all-gather.11.cloned.1.call-done
  3327.0 159.5 %fusion.26 = bf16[16,512,2048]{2,1,0:T(8,128)(2,1)} fusion(f32[16,512,4096]{2,1,0:T(8,128)} %reshape.272, f32[16,512,4096]{2,1,0:T(8,128)} %reshape.271, bf16[4096,2048]{1,0:T(8,128)(2,1)} %all-gather.11.cloned.1.call-done), kind=kOutput, calls=%fused_computation.35 | convolution fusion | flops 137657057280 | bytes 318767104 | tf_op jit(solution)/shard_map/bsf,fd->bsd/dot_general | solution.py:82
  3486.5 0.0 all-reduce.5.cloned.1.call-update
  3486.5 0.0 copy-start.3
  3486.6 16.6 copy.31
  3503.2 8.9 fusion.49
  3512.1 6.4 copy.36
  3518.5 6.4 copy.35
  3524.9 6.4 copy.34
  3531.3 0.0 copy-done.3
  3531.3 36.1 broadcast_select_fusion
  3567.4 54.3 %reshape.269 = bf16[2048,4,2,1024]{3,2,1,0:T(2,128)(2,1)} reshape(bf16[2048,8192]{1,0:T(8,128)(2,1)} %all-gather.9.cloned.1.call-done) | data formatting | bytes 67108864 | tf_op jit(solution)/shard_map/reshape | solution.py:48
  3621.7 97.6 %fusion.48 = (bf16[2048,4,1,1024]{3,2,1,0:T(2,128)(2,1)}, bf16[2048,4,1,1024]{3,2,1,0:T(2,128)(2,1)}) fusion(bf16[2048,4,2,1024]{3,2,1,0:T(2,128)(2,1)} %reshape.269), kind=kLoop, calls=%fused_computation.73 | loop fusion | bytes 67108864 | tf_op jit(solution)/shard_map/slice | solution.py:50
  3719.3 75.9 %copy.45 = bf16[2048,4,1,1024]{0,3,1,2:T(8,128)(2,1)} copy(bf16[2048,4,1,1024]{3,2,1,0:T(2,128)(2,1)} %get-tuple-element.28) | data formatting | bytes 33554432
  3795.3 21.2 copy.38
  3816.5 75.9 %copy.44 = bf16[2048,4,1,1024]{0,3,1,2:T(8,128)(2,1)} copy(bf16[2048,4,1,1024]{3,2,1,0:T(2,128)(2,1)} %get-tuple-element.29) | data formatting | bytes 33554432
  3892.4 21.2 copy.37
  3913.6 304.9 %all-reduce.5.cloned.1.call-done = bf16[16,512,2048]{2,1,0:T(8,128)(2,1)} async-done(((bf16[16,512,2048]{2,1,0:T(8,128)(2,1)}), bf16[16,512,2048]{2,1,0:T(8,128)(2,1)}) %all-reduce.5.cloned.1.call-update) | async-done | bytes 33554448 | tf_op jit(solution)/shard_map/psum | solution.py:83
  4218.5 43.3 %fusion.13 = bf16[16,512,2048]{2,1,0:T(8,128)(2,1)} fusion(bf16[16,512,2048]{2,1,0:T(8,128)(2,1)} %all-reduce.5.cloned.1.call-done, bf16[16,512,2048]{2,1,0:T(8,128)(2,1)} %all-reduce.3.cloned.1.call-done, bf16[16,512,2048]{2,1,0:T(8,128)(2,1)} %param.10), kind=kLoop, calls=%fused_computation.26 | loop fusion | flops 134217728 | bytes 134217728 | tf_op jit(solution)/shard_map/convert_element_type | solution.py:84
  4261.8 4.8 copy.50
  4266.6 14.2 copy.51
  (5 shorter events, 0.1 us)
Async XLA Ops:
  7.2 85.2 %all-gather.5.cloned.1.call-start = ((), (), s32[]{:S(2)}) async-start(), calls=%async_computation | async-start | bytes 15728640 | tf_op jit(solution)/shard_map/all_gather | solution.py:95
  7.9 614.2 %all-gather.7.cloned.1.call-start = ((), (), s32[]{:S(2)}) async-start(), calls=%async_computation.1 | async-start | bytes 5242880 | tf_op jit(solution)/shard_map/all_gather | solution.py:96
  8.7 1391.2 %all-reduce.3.cloned.1.call-start = ((), (), s32[]{:S(2)}) async-start(), calls=%async_computation.2 | async-start | bytes 67108864 | tf_op jit(solution)/shard_map/psum | solution.py:74
  9.5 13.0 copy-start.2
  265.9 34.0 copy-start
  265.9 34.0 copy-start.1
  667.8 1.2 copy-start.4
  667.9 934.1 %all-gather.9.cloned.1.call-start = ((), (), s32[]{:S(2)}) async-start(), calls=%async_computation.3 | async-start | bytes 41943040 | tf_op jit(solution)/shard_map/all_gather | solution.py:97
  668.4 2658.6 %all-gather.11.cloned.1.call-start = ((), (), s32[]{:S(2)}) async-start(), calls=%async_computation.4 | async-start | bytes 20971520 | tf_op jit(solution)/shard_map/all_gather | solution.py:98
  669.0 3549.5 %all-reduce.5.cloned.1.call-start = ((), (), s32[]{:S(2)}) async-start(), calls=%async_computation.5 | async-start | bytes 67108864 | tf_op jit(solution)/shard_map/psum | solution.py:83
  3486.5 44.7 %copy-start.3 = (pred[16,512]{1,0:T(8,128)(4,1)S(1)}, pred[16,512]{1,0:T(8,128)(4,1)}, u32[]{:S(2)}) copy-start(pred[16,512]{1,0:T(8,128)(4,1)} %copy-done.2) | copy-start | bytes 24580
Sparse Core Ops, SparseCore 0:
  9.5 82.7 all-gather.4
  93.9 31.4 all-gather.6
  668.0 731.7 all-reduce.2
  1401.2 200.7 all-gather.8
  1603.4 104.1 all-gather.10
  3486.7 731.7 all-reduce.4
where the time goes:
time: 4320 us; the launch traced here: 4290 us
  waiting for transfers between devices  1290 us (30%)
  other arithmetic  1180 us (27%)
  local copies, waits for them, and re-layouts  993 us (23%)
  matrix products  818 us (19%)
    convert_element_type x1, other arithmetic, prefill(): gu_act[..., 0, :].astype(jnp.float32)  908 us
    psum x1, waiting for transfers between devices, prefill(): attn_sum = lax.psum(attn_part, 'tpa')  731 us
    psum x1, waiting for transfers between devices, prefill(): mlp_sum = lax.psum(mlp_part, 'tpa')  305 us
    dot_general x1, matrix products, prefill(): jnp.einsum('bsd,dc->bsc', h_normed, gu_cols, preferred_element_type=jnp.f...  293 us
    unnamed x19, local copies, waits for them, and re-layouts  232 us
    reshape x1, local copies, waits for them, and re-layouts, prefill(): gu_act = gu_act.reshape(batch_loc, seq_len, n_tpb, 2, ff_block)  213 us
    all_gather x1, waiting for transfers between devices, local_step(): gu_cols = lax.all_gather(w_gate_up, 'tpb', axis=1, tiled=True)  181 us
    dot_general x1, matrix products, prefill(): jnp.einsum('bsf,fd->bsd', mid_act, down_rows, preferred_element_type=jnp....  160 us
  transfers between devices with their start and end apart: 6, of which 4 were waited for; matrix products, arithmetic and copies ran while one was open for 63% of the time, Pallas kernels for 0%

commit v1 on v0

v1 whole, which is shorter than its diff:
```python
import functools
import math
import jax
import jax.numpy as jnp
from jax import lax
from jax.experimental import pallas as pl
from jax.experimental.layout import Layout, with_layout_constraint
from jax.experimental.pallas import tpu as pltpu
from jax.sharding import PartitionSpec as P

ROPE_BASE = 500000.0
ROPE_FACTOR = 8.0
LOW_FREQ = 1.0
HIGH_FREQ = 4.0
ORIG_CONTEXT = 8192.0
NORM_EPS = 1e-5
MASK_VALUE = -1e30
BF16 = jnp.bfloat16
F32 = jnp.float32
SHARED = 0
CHUNK = 2


def rms_norm(x_in, gain_vec):
    x_wide = x_in.astype(F32)
    mean_sq = jnp.mean(x_wide * x_wide, axis=-1, keepdims=True)
    return (x_wide * lax.rsqrt(mean_sq + NORM_EPS) * gain_vec.astype(F32)).astype(BF16)


def rope_angles(seq_len, head_dim):
    exponent = jnp.arange(head_dim // 2, dtype=F32) * (2.0 / head_dim)
    inv_freq = 1.0 / jnp.power(ROPE_BASE, exponent)
    wavelen = 2.0 * math.pi / inv_freq
    smooth = (ORIG_CONTEXT / wavelen - LOW_FREQ) / (HIGH_FREQ - LOW_FREQ)
    blended = (1.0 - smooth) * inv_freq / ROPE_FACTOR + smooth * inv_freq
    freq = jnp.where(wavelen < ORIG_CONTEXT / HIGH_FREQ, inv_freq, jnp.where(wavelen > ORIG_CONTEXT / LOW_FREQ, inv_freq / ROPE_FACTOR, blended))
    return jnp.arange(seq_len, dtype=F32)[:, None] * freq[None, :]


def matmul(lhs, rhs):
    return jnp.einsum('bsd,dc->bsc', lhs, rhs, preferred_element_type=F32)


def matmul_t(lhs, rhs):
    prod = with_layout_constraint(matmul(lhs, rhs), Layout((0, 2, 1)))
    return jnp.transpose(prod, (0, 2, 1)).astype(BF16)


def rope_rows(first, second, cos_t, sin_t):
    return first * cos_t - second * sin_t, second * cos_t + first * sin_t


def attn_kernel(len_ref, q_ref, k_ref, v_ref, cos_ref, sin_ref, cos_t_ref, sin_t_ref, o_ref, *, half, blk):
    seq = q_ref.shape[1]
    hd = 2 * half
    length = len_ref[pl.program_id(0)]
    cos_t, sin_t = cos_t_ref[...], sin_t_ref[...]
    keys = []
    for h in range(2):
        k_first = k_ref[0, h * hd:h * hd + half, :].astype(F32)
        k_second = k_ref[0, h * hd + half:(h + 1) * hd, :].astype(F32)
        lo, hi = rope_rows(k_first, k_second, cos_t, sin_t)
        keys.append(jnp.concatenate([lo, hi], axis=0).astype(BF16))
    for i in range(seq // blk):
        rows = slice(i * blk, (i + 1) * blk)
        width = (i + 1) * blk
        q_in = q_ref[0, rows, :].astype(F32)
        lane = lax.broadcasted_iota(jnp.int32, q_in.shape, 1)
        swapped = jnp.where(lane % hd < half, pltpu.roll(q_in, 2 * hd - half, 1), pltpu.roll(q_in, half, 1))
        q_rot = (q_in * cos_ref[rows, :] + swapped * sin_ref[rows, :]).astype(BF16) * BF16(hd ** -0.5)
        row = lax.broadcasted_iota(jnp.int32, (blk, width), 0) + i * blk
        col = lax.broadcasted_iota(jnp.int32, (blk, width), 1)
        allowed = col <= jnp.minimum(row, length - 1)
        outs = []
        for h in range(2):
            scores = jnp.dot(q_rot[:, h * hd:(h + 1) * hd], keys[h][:, :width], preferred_element_type=F32)
            scores = jnp.where(allowed, scores, MASK_VALUE)
            expd = jnp.exp(scores - jnp.max(scores, axis=-1, keepdims=True))
            prob = (expd * (1.0 / jnp.sum(expd, axis=-1, keepdims=True))).astype(BF16)
            outs.append(lax.dot_general(prob, v_ref[0, :, :width], (((1,), (1,)), ((), ())), preferred_element_type=F32))
        o_ref[0, rows, :] = jnp.where(lane < hd, outs[0], outs[1]).astype(BF16)


def attention(lengths, q, k_t, v_t, angles):
    batch, seq, width = q.shape
    half = angles.shape[1]
    hd = 2 * half
    cos, sin = jnp.cos(angles), jnp.sin(angles)
    cos_row = jnp.tile(jnp.concatenate([cos, cos], axis=1), (1, 2))
    sin_row = jnp.tile(jnp.concatenate([-sin, sin], axis=1), (1, 2))
    whole = lambda shape: pl.BlockSpec(shape, lambda b, j, *_: (0, 0))
    return pl.pallas_call(
        functools.partial(attn_kernel, half=half, blk=256),
        grid_spec=pltpu.PrefetchScalarGridSpec(
            num_scalar_prefetch=1,
            grid=(batch, width // (2 * hd)),
            in_specs=[
                pl.BlockSpec((1, seq, 2 * hd), lambda b, j, *_: (b, 0, j)),
                pl.BlockSpec((1, 2 * hd, seq), lambda b, j, *_: (b, j, 0)),
                pl.BlockSpec((1, 2 * hd, seq), lambda b, j, *_: (b, j, 0)),
                whole((seq, 2 * hd)), whole((seq, 2 * hd)), whole((half, seq)), whole((half, seq)),
            ],
            out_specs=pl.BlockSpec((1, seq, 2 * hd), lambda b, j, *_: (b, 0, j)),
        ),
        out_shape=jax.ShapeDtypeStruct(q.shape, BF16),
        compiler_params=pltpu.CompilerParams(dimension_semantics=("parallel", "arbitrary")),
        cost_estimate=pl.CostEstimate(flops=batch * width * seq * seq * 16, bytes_accessed=8 * q.size, transcendentals=0),
        name="prefill_attention",
    )(lengths, q, k_t, v_t, cos_row, sin_row, cos.T, sin.T)


def cache_kernel(pos_ref, len_ref, k_own, v_own, k_oth, v_oth, k_buf, v_buf, cos_ref, sin_ref, k_out, v_out, *, n_own):
    prompt = pl.program_id(0)
    local = prompt - pos_ref[0]
    is_own = (local >= 0) & (local < n_own)
    half, seq = cos_ref.shape
    valid = lax.broadcasted_iota(jnp.int32, (half, seq), 1) < len_ref[prompt]

    def emit(k_ref, v_ref):
        cos_t, sin_t = cos_ref[...], sin_ref[...]
        for h in range(k_out.shape[1]):
            first = k_ref[0, h, :half, :].astype(F32)
            second = k_ref[0, h, half:, :].astype(F32)
            lo, hi = rope_rows(first, second, cos_t, sin_t)
            k_out[0, h, :half, :] = jnp.where(valid, lo, k_buf[0, h, :half, :].astype(F32)).astype(BF16)
            k_out[0, h, half:, :] = jnp.where(valid, hi, k_buf[0, h, half:, :].astype(F32)).astype(BF16)
            for part in (slice(0, half), slice(half, 2 * half)):
                v_out[0, h, part, :] = jnp.where(valid, v_ref[0, h, part, :].astype(F32), v_buf[0, h, part, :].astype(F32)).astype(BF16)

    @pl.when(is_own)
    def _():
        emit(k_own, v_own)

    @pl.when(jnp.logical_not(is_own))
    def _():
        emit(k_oth, v_oth)


def fill_cache(pos, lengths, k_own, v_own, k_oth, v_oth, k_buf, v_buf, angles):
    batch, heads, hd, seq = k_buf.shape
    n_own, n_oth = k_own.shape[0], k_oth.shape[0]
    blk = 8
    steps = heads // blk

    def own_map(p, j, pos, _):
        local = p - pos[0]
        inside = (local >= 0) & (local < n_own)
        return (jnp.clip(local, 0, n_own - 1), pos[2] * steps + jnp.where(inside, j, jnp.where(local < 0, 0, steps - 1)), 0, 0)

    def oth_map(p, j, pos, _):
        local = p - pos[1]
        inside = (local >= 0) & (local < n_oth)
        return (jnp.clip(local, 0, n_oth - 1), jnp.where(inside, j, jnp.where(local < 0, 0, steps - 1)), 0, 0)

    shape = (1, blk, hd, seq)
    plain = pl.BlockSpec(shape, lambda p, j, *_: (p, j, 0, 0))
    table = pl.BlockSpec((hd // 2, seq), lambda p, j, *_: (0, 0))
    out = jax.ShapeDtypeStruct(k_buf.shape, BF16)
    return pl.pallas_call(
        functools.partial(cache_kernel, n_own=n_own),
        grid_spec=pltpu.PrefetchScalarGridSpec(
            num_scalar_prefetch=2,
            grid=(batch, steps),
            in_specs=[pl.BlockSpec(shape, own_map), pl.BlockSpec(shape, own_map), pl.BlockSpec(shape, oth_map), pl.BlockSpec(shape, oth_map), plain, plain, table, table],
            out_specs=[plain, plain],
        ),
        out_shape=[out, out],
        compiler_params=pltpu.CompilerParams(dimension_semantics=("arbitrary", "arbitrary")),
        cost_estimate=pl.CostEstimate(flops=40 * 10**9, bytes_accessed=12 * k_buf.size, transcendentals=0),
        name="fill_cache",
    )(pos, lengths, k_own, v_own, k_oth, v_oth, k_buf, v_buf, jnp.cos(angles).T, jnp.sin(angles).T)


def unpack_qkv(w_qkv, head_dim):
    cols = w_qkv.shape[1]
    third = cols // 3
    out_col = jnp.arange(cols)
    kind, rest = out_col // third, out_col % third
    source = (rest // head_dim) * 3 * head_dim + kind * head_dim + rest % head_dim
    select = (jnp.arange(cols)[:, None] == source[None, :]).astype(BF16)
    plain = jnp.dot(w_qkv, select, preferred_element_type=F32).astype(BF16)
    return plain[:, :third], plain[:, third:2 * third], plain[:, 2 * third:]


def solution(mesh):
    n_tpa = mesh.shape['tpa']

    def local_step(x_loc, len_loc, k_buf, v_buf, w_qkv, w_o, w_gate_up, w_down, g_attn, g_mlp):
        batch, seq, _ = x_loc.shape
        heads, head_dim = k_buf.shape[2:]
        n_oth = batch // n_tpa - SHARED // 2
        n_own = batch - n_oth
        mine = lax.axis_index('tpa')
        own_at, oth_at = mine * n_oth, (1 - mine) * n_own
        axes = ('tpa', 'tpb')
        take = lambda arr, at, n, axis=0: lax.dynamic_slice_in_dim(arr, at, n, axis)
        cols = lambda w: lax.all_gather(w, axes, axis=1, tiled=True)
        rows = lambda w: lax.all_gather(w, axes, axis=0, tiled=True)

        wq, wk, wv = unpack_qkv(w_qkv, head_dim)
        ff = w_gate_up.shape[1] // 2
        wk, wv, wq = cols(wk), cols(wv), cols(wq)
        wo = rows(w_o)
        wgate, wup = cols(w_gate_up[:, :ff]), cols(w_gate_up[:, ff:])
        wdown = rows(w_down)
        share = lambda w, axis: take(w, mine * (w.shape[axis] // n_tpa), w.shape[axis] // n_tpa, axis)
        out_w = (share(wq, 1), share(wk, 1), share(wv, 1), share(wo, 0), share(wgate, 1), share(wup, 1), share(wdown, 0))

        angles = rope_angles(seq, head_dim)
        u = rms_norm(x_loc, g_attn)
        x_own, u_own, u_oth = take(x_loc, own_at, n_own), take(u, own_at, n_own), take(u, oth_at, n_oth)
        len_own = take(len_loc, own_at, n_own)
        k_t, v_t = matmul_t(u_own, wk), matmul_t(u_own, wv)
        q = matmul(u_own, wq).astype(BF16)
        k_oth, v_oth = matmul_t(u_oth, out_w[1]), matmul_t(u_oth, out_w[2])
        attn = attention(len_own, q, k_t, v_t, angles)
        hidden = (x_own.astype(F32) + matmul(attn, wo)).astype(BF16)
        u2 = rms_norm(hidden, g_mlp)
        gate = matmul(u2, wgate).astype(BF16)
        up = matmul(u2, wup).astype(BF16)
        mid = (jax.nn.silu(gate.astype(F32)) * up.astype(F32)).astype(BF16)

        heads_of = lambda t: t.reshape(t.shape[0], t.shape[1] // head_dim, head_dim, seq)
        turn = lambda t: jnp.transpose(t, (0, 2, 3, 1))
        pos = jnp.stack([own_at, oth_at, mine]).astype(jnp.int32)
        k_cache, v_cache = fill_cache(pos, len_loc, heads_of(k_t), heads_of(v_t), heads_of(k_oth), heads_of(v_oth), turn(k_buf), turn(v_buf), angles)
        back = lambda t: jnp.transpose(t, (0, 3, 1, 2))

        swap = [(i, n_tpa - 1 - i) for i in range(n_tpa)]
        y_out = jnp.zeros(x_loc.shape, BF16)
        sent_at = mine * (n_own - n_oth)
        for start in range(0, n_oth, CHUNK):
            n = min(CHUNK, n_oth - start)
            local = sent_at + start
            part = (take(hidden, local, n).astype(F32) + matmul(take(mid, local, n), wdown)).astype(BF16)
            other = lax.ppermute(part, 'tpa', swap)
            y_out = lax.dynamic_update_slice_in_dim(y_out, part, own_at + local, 0)
            y_out = lax.dynamic_update_slice_in_dim(y_out, other, oth_at + start, 0)
        return (y_out, back(k_cache), back(v_cache)) + out_w

    batch_spec = P(('part', 'tpb'), None, None)
    len_spec = P(('part', 'tpb'))
    cache_spec = P(('part', 'tpb'), None, 'tpa', None)
    train_cols = P('part', ('tpa', 'tpb'))
    train_rows = P(('part', 'tpa', 'tpb'), None)
    gain_spec = P('part')
    gen_cols = P('part', 'tpa')
    gen_rows = P(('part', 'tpa'), None)
    return jax.shard_map(local_step, mesh=mesh, in_specs=(batch_spec, len_spec, cache_spec, cache_spec, train_cols, train_rows, train_cols, train_rows, gain_spec, gain_spec), out_specs=(batch_spec, cache_spec, cache_spec, gen_cols, gen_cols, gen_cols, gen_rows, gen_cols, gen_cols, gen_rows), check_vma=False)
```

time: 4320 us -> 1350 us (0.31)
  other arithmetic: 1180 us -> 37.1 us
  waiting for transfers between devices: 1290 us -> 219 us
  local copies, waits for them, and re-layouts: 993 us -> 115 us
  Pallas kernels: 0 us -> 236 us
  matrix products: 818 us -> 714 us
    psum x2 -> x0, waiting for transfers between devices: 1040 us -> none  [the longest x1 731 us: prefill(): attn_sum = lax.psum(attn_part, 'tpa')]
    convert_element_type x5 -> x3, other arithmetic: 986 us -> 23.8 us  [the longest x1 23.2 us: rms_norm(): (x_wide * lax.rsqrt(mean_sq + NORM_EPS) * gain_vec.astype(F32)).astype(BF16)]
    convert_element_type x3 -> x0, local copies, waits for them, and re-layouts: 370 us -> none  [the longest x1 155 us: prefill(): gu_act[..., 1, :].astype(jnp.float32)]
    reshape x2 -> x0, local copies, waits for them, and re-layouts: 267 us -> none  [the longest x1 213 us: prefill(): gu_act = gu_act.reshape(batch_loc, seq_len, n_tpb, 2, ff_block)]
    pallas_call x0 -> x2, Pallas kernels: none -> 236 us  [the longest x1 191 us: attention(): pl.pallas_call(functools.partial(attn_kernel, half=half, blk=256), grid_s...]
    all_gather x4 -> x7, waiting for transfers between devices: 247 us -> 20.5 us  [the longest x5 20.5 us: local_step(): cols = lambda w: lax.all_gather(w, axes, axis=1, tiled=True)]
    unnamed x19 -> x35, local copies, waits for them, and re-layouts: 232 us -> 21.1 us
    ppermute x0 -> x4, waiting for transfers between devices: none -> 196 us  [local_step(): other = lax.ppermute(part, 'tpa', swap)]
  transfers between devices with their start and end apart: 6 -> 11, of which waited for: 4 -> 6; matrix products, arithmetic and copies ran while one was open for 63% -> 49% of each run, Pallas kernels for 0% -> 18%
where the time goes in v1:
time: 1350 us; the launch traced here: 1340 us
  matrix products  714 us (53%)
  Pallas kernels  236 us (17%)
  waiting for transfers between devices  219 us (16%)
  local copies, waits for them, and re-layouts  115 us (9%)
  other arithmetic  37.1 us (3%)
  between operations  14.8 us (1%)
    dot_general x12, matrix products, matmul(): return jnp.einsum('bsd,dc->bsc', lhs, rhs, preferred_element_type=F32)  712 us
    ppermute x4, waiting for transfers between devices, local_step(): other = lax.ppermute(part, 'tpa', swap)  196 us
    pallas_call x1, Pallas kernels, attention(): pl.pallas_call(functools.partial(attn_kernel, half=half, blk=256), grid_s...  191 us
    dynamic_slice x8, local copies, waits for them, and re-layouts, local_step(): take = lambda arr, at, n, axis=0: lax.dynamic_slice_in_dim(arr, at, n, axis)  57.1 us
    pallas_call x1, Pallas kernels, fill_cache(): pl.pallas_call(functools.partial(cache_kernel, n_own=n_own), grid_spec=pl...  44.6 us
  transfers between devices with their start and end apart: 11, of which 6 were waited for; matrix products, arithmetic and copies ran while one was open for 49% of the time, Pallas kernels for 18%

profile of v1, /device:TPU:0, one launch (start us, length us, event | category | flops | bytes accessed | tf_op | source)
XLA Modules:
  0.0 1342.7 jit_solution(14635497407337110740)
XLA Ops:
  7.2 0.0 all-gather.10.cloned.1.call-start
  7.3 1.8 copy-done
  9.1 2.9 fusion.51
  12.0 1.7 fusion.84
  13.7 0.0 all-gather.12.cloned.1.call-start
  13.8 0.7 all-gather.12.cloned.1.call-update
  14.5 0.0 all-gather.8.cloned.1.call-start
  14.5 0.7 all-gather.8.cloned.1.call-update
  15.2 0.0 all-gather.14.cloned.1.call-start
  15.3 0.5 all-gather.14.cloned.1.call-update
  15.8 0.0 all-gather.16.cloned.1.call-start
  15.8 6.0 fusion.83
  21.9 0.0 all-gather.18.cloned.1.call-start
  22.0 0.5 all-gather.18.cloned.1.call-update
  22.5 0.5 all-gather.20.cloned.1.call-start
  23.0 0.2 all-gather.20.cloned.1.call-update
  23.3 1.0 fusion.55
  24.2 0.3 fusion.59
  24.6 0.6 convert_element_type.109
  25.2 11.3 fusion.5
  36.6 0.8 copy.23.cos_ref
  37.4 0.8 copy.24.sin_ref
  38.3 0.7 dynamic_slice.58.len_ref
  38.9 23.2 %fusion.7 = bf16[16,512,2048]{2,1,0:T(8,128)(2,1)} fusion(bf16[16,512,2048]{2,1,0:T(8,128)(2,1)} %param.10, f32[2048]{0:T(1024)S(1)} %convert_element_type.97, f32[16,512]{1,0:T(8,128)S(1)} %add_rsqrt_fusion), kind=kLoop, calls=%fused_computation.11 | loop fusion | flops 67108864 | bytes 67149824 | tf_op jit(solution)/shard_map/convert_element_type | solution.py:27
  62.1 3.0 all-gather.10.cloned.1.call-done
  65.1 42.0 %convolution_convert_fusion.1 = bf16[8,512,2048]{1,2,0:T(8,128)(2,1)} fusion(bf16[16,512,2048]{2,1,0:T(8,128)(2,1)} %fusion.7, s32[]{:T(128)S(6)} %select_n.117, bf16[2048,2048]{0,1:T(8,128)(2,1)} %all-gather.10.cloned.1.call-done), kind=kOutput, calls=%fused_computation.34 | convolution fusion | flops 34368126976 | bytes 41943044 | tf_op jit(solution)/shard_map/bsd,dc->bsc/dot_general | solution.py:41
  107.1 8.8 all-gather.12.cloned.1.call-done
  115.8 42.0 %convolution_convert_fusion = bf16[8,512,2048]{1,2,0:T(8,128)(2,1)} fusion(bf16[16,512,2048]{2,1,0:T(8,128)(2,1)} %fusion.7, s32[]{:T(128)S(6)} %select_n.117, bf16[2048,2048]{0,1:T(8,128)(2,1)} %all-gather.12.cloned.1.call-done), kind=kOutput, calls=%fused_computation.33 | convolution fusion | flops 34368126976 | bytes 41943044 | tf_op jit(solution)/shard_map/bsd,dc->bsc/dot_general | solution.py:41
  157.8 8.8 all-gather.8.cloned.1.call-done
  166.6 41.9 %convolution_convert_fusion.2.q_ref = bf16[8,512,2048]{2,1,0:T(8,128)(2,1)} fusion(bf16[16,512,2048]{2,1,0:T(8,128)(2,1)} %fusion.7, s32[]{:T(128)S(6)} %select_n.117, bf16[2048,2048]{0,1:T(8,128)(2,1)} %all-gather.8.cloned.1.call-done), kind=kOutput, calls=%fused_computation.35 | convolution fusion | flops 34368126976 | bytes 41943044 | tf_op jit(solution)/shard_map/bsd,dc->bsc/dot_general | solution.py:41
  208.4 191.5 %prefill_attention.1 = bf16[8,512,2048]{2,1,0:T(8,128)(2,1)} custom-call(s32[8]{0:T(128)} %dynamic_slice.58.len_ref, bf16[8,512,2048]{2,1,0:T(8,128)(2,1)} %convolution_convert_fusion.2.q_ref, bf16[8,2048,512]{2,1,0:T(8,128)(2,1)} %bitcast.88, bf16[8,2048,512]{2,1,0:T(8,128)(2,1)} %bitcast.90, f32[512,128]{1,0:T(8,128)} %copy.23.cos_ref, ...), custom_call_target="tpu_custom_call" | custom-call | flops 68719476736 | bytes 67108864 | tf_op jit(solution)/shard_map/prefill_attention/pallas_call | solution.py:92
  400.0 44.0 %fusion.8 = (f32[8,512]{1,0:T(8,128)S(1)}, bf16[8,512,2048]{2,1,0:T(8,128)(2,1)}) fusion(bf16[8,512,2048]{2,1,0:T(8,128)(2,1)} %prefill_attention.1, bf16[2048,2048]{1,0:T(8,128)(2,1)} %all-gather.14.cloned.1.call-done, bf16[16,512,2048]{2,1,0:T(8,128)(2,1)} %param.10, s32[]{:T(128)S(6)} %select_n.117), kind=kOutput, calls=%fused_computation.14 | convolution fusion | flops 34410065920 | bytes 58736644 | tf_op jit(solution)/shard_map/bsd,dc->bsc/dot_general | solution.py:41
  444.0 154.9 %fusion.20 = bf16[8,512,8192]{2,1,0:T(8,128)(2,1)} fusion(bf16[2048,8192]{1,0:T(8,128)(2,1)} %all-gather.16.cloned.1.call-done, bf16[8,512,2048]{2,1,0:T(8,128)(2,1)} %get-tuple-element.45, f32[2048]{0:T(1024)S(1)} %copy-done.4, f32[8,512]{1,0:T(8,128)S(1)} %add_rsqrt_fusion.1), kind=kOutput, calls=%fused_computation.26 | convolution fusion | flops 137472507904 | bytes 117465088 | tf_op jit(solution)/shard_map/bsd,dc->bsc/dot_general | solution.py:41
  598.9 160.7 %fusion.4 = bf16[8,512,8192]{2,1,0:T(8,128)(2,1)} fusion(bf16[8,512,8192]{2,1,0:T(8,128)(2,1)} %fusion.20, bf16[2048,8192]{1,0:T(8,128)(2,1)} %all-gather.18.cloned.1.call-done, bf16[8,512,2048]{2,1,0:T(8,128)(2,1)} %get-tuple-element.45, f32[2048]{0:T(1024)S(1)} %copy-done.4, f32[8,512]{1,0:T(8,128)S(1)} %add_rsqrt_fusion.1), kind=kOutput, calls=%fused_computation.6 | convolution fusion | flops 137774497792 | bytes 184573952 | tf_op jit(solution)/shard_map/bsd,dc->bsc/dot_general | solution.py:41
  759.6 11.2 broadcast_in_dim.2
  770.8 45.2 %constant_dynamic-update-slice_fusion.7 = (bf16[16,512,2048]{2,1,0:T(8,128)(2,1)}, bf16[2,512,2048]{2,1,0:T(8,128)(2,1)}) fusion(bf16[16,512,2048]{2,1,0:T(8,128)(2,1)} %broadcast_in_dim.2, s32[]{:T(128)S(6)} %select_n.117, bf16[8,512,8192]{2,1,0:T(8,128)(2,1)} %fusion.4, bf16[8192,2048]{1,0:T(8,128)(2,1)} %all-gather.20.cloned.1.call-done, ...), kind=kOutput, calls=%fused_computation.98 | convolution fusion | flops 34366029824 | bytes 113246208 | tf_op jit(solution)/shard_map/bsd,dc->bsc/dot_general | solution.py:41
  816.0 1.4 collective-permute-start
  817.4 91.3 %collective-permute-done = bf16[2,512,2048]{2,1,0:T(8,128)(2,1)} collective-permute-done((bf16[2,512,2048]{2,1,0:T(8,128)(2,1)}, bf16[2,512,2048]{2,1,0:T(8,128)(2,1)}, u32[]{:S(2)}, u32[]{:S(2)}) %collective-permute-start) | collective-permute-done | bytes 4194336 | tf_op jit(solution)/shard_map/ppermute | solution.py:236
  908.7 4.8 constant_dynamic-update-slice_fusion.6
  913.5 45.0 %constant_dynamic-update-slice_fusion.5 = (bf16[16,512,2048]{2,1,0:T(8,128)(2,1)}, bf16[2,512,2048]{2,1,0:T(8,128)(2,1)}) fusion(bf16[16,512,2048]{2,1,0:T(8,128)(2,1)} %constant_dynamic-update-slice_fusion.6, s32[]{:T(128)S(6)} %select_n.125, bf16[8,512,8192]{2,1,0:T(8,128)(2,1)} %fusion.4, bf16[8192,2048]{1,0:T(8,128)(2,1)} %all-gather.20.cloned.1.call-done, ...), kind=kOutput, calls=%fused_computation.96 | convolution fusion | flops 34366029824 | bytes 113246208 | tf_op jit(solution)/shard_map/bsd,dc->bsc/dot_general | solution.py:41
  958.6 1.4 collective-permute-start.1
  959.9 0.7 pad_add_fusion.pos_ref
  960.6 2.5 constant_dynamic-slice_fusion.6
  963.1 4.0 constant_dynamic-slice_fusion.5
  967.1 23.6 %fusion.38 = bf16[8,512,1024]{1,2,0:T(8,128)(2,1)} fusion(bf16[16,512,2048]{2,1,0:T(8,128)(2,1)} %fusion.7, s32[]{:T(128)S(6)} %select_n.124, bf16[2048,1024]{0,1:T(8,128)(2,1)S(1)} %constant_dynamic-slice_fusion.5), kind=kOutput, calls=%fused_computation.48 | convolution fusion | flops 17184063488 | bytes 29360132 | tf_op jit(solution)/shard_map/bsd,dc->bsc/dot_general | solution.py:41
  990.8 59.8 %collective-permute-done.1 = bf16[2,512,2048]{2,1,0:T(8,128)(2,1)} collective-permute-done((bf16[2,512,2048]{2,1,0:T(8,128)(2,1)}, bf16[2,512,2048]{2,1,0:T(8,128)(2,1)}, u32[]{:S(2)}, u32[]{:S(2)}) %collective-permute-start.1) | collective-permute-done | bytes 4194336 | tf_op jit(solution)/shard_map/ppermute | solution.py:236
  1050.5 4.8 constant_dynamic-update-slice_fusion.4
  1055.3 45.1 %constant_dynamic-update-slice_fusion.3 = (bf16[16,512,2048]{2,1,0:T(8,128)(2,1)}, bf16[2,512,2048]{2,1,0:T(8,128)(2,1)}) fusion(bf16[16,512,2048]{2,1,0:T(8,128)(2,1)} %constant_dynamic-update-slice_fusion.4, s32[]{:T(128)S(6)} %select_n.127, bf16[8,512,8192]{2,1,0:T(8,128)(2,1)} %fusion.4, bf16[8192,2048]{1,0:T(8,128)(2,1)} %all-gather.20.cloned.1.call-done, ...), kind=kOutput, calls=%fused_computation.94 | convolution fusion | flops 34366029824 | bytes 113246208 | tf_op jit(solution)/shard_map/bsd,dc->bsc/dot_general | solution.py:41
  1100.4 1.4 collective-permute-start.2
  1101.7 22.0 %fusion.35 = bf16[8,512,1024]{1,2,0:T(8,128)(2,1)} fusion(bf16[16,512,2048]{2,1,0:T(8,128)(2,1)} %fusion.7, s32[]{:T(128)S(6)} %select_n.124, bf16[2048,1024]{0,1:T(8,128)(2,1)S(1)} %constant_dynamic-slice_fusion.6), kind=kOutput, calls=%fused_computation.47 | convolution fusion | flops 17184063488 | bytes 29360132 | tf_op jit(solution)/shard_map/bsd,dc->bsc/dot_general | solution.py:41
  1123.8 6.4 copy.27
  1130.2 6.4 copy.26
  1136.6 4.8 constant_dynamic-slice_fusion.4
  1141.3 6.4 copy.25
  1147.7 44.6 %fill_cache.1 = (bf16[16,16,64,512]{3,2,1,0:T(8,128)(2,1)}, bf16[16,16,64,512]{3,2,1,0:T(8,128)(2,1)}) custom-call(s32[3]{0:T(128)} %pad_add_fusion.pos_ref, s32[16]{0:T(128)} %len_ref.1, bf16[8,32,64,512]{3,2,1,0:T(8,128)(2,1)} %bitcast.89, bf16[8,32,64,512]{3,2,1,0:T(8,128)(2,1)} %bitcast.91, bf16[8,16,64,512]{3,2,1,0:T(8,128)(2,1)} %bitcast.95, ...), custom_call_target="tpu_custom_call" | custom-call | flops 40000000000 | bytes 100663296 | tf_op jit(solution)/shard_map/fill_cache/pallas_call | solution.py:159
  1192.4 4.8 constant_dynamic-update-slice_fusion.2
  1197.1 45.1 %constant_dynamic-update-slice_fusion.1 = (bf16[16,512,2048]{2,1,0:T(8,128)(2,1)}, bf16[2,512,2048]{2,1,0:T(8,128)(2,1)}) fusion(bf16[16,512,2048]{2,1,0:T(8,128)(2,1)} %constant_dynamic-update-slice_fusion.2, s32[]{:T(128)S(6)} %select_n.129, bf16[8,512,8192]{2,1,0:T(8,128)(2,1)} %fusion.4, bf16[8192,2048]{1,0:T(8,128)(2,1)} %all-gather.20.cloned.1.call-done, ...), kind=kOutput, calls=%fused_computation.92 | convolution fusion | flops 34366029824 | bytes 113246208 | tf_op jit(solution)/shard_map/bsd,dc->bsc/dot_general | solution.py:41
  1242.2 0.7 collective-permute-start.3
  1242.9 4.8 constant_dynamic-slice_fusion.3
  1247.7 17.0 %constant_dynamic-slice_fusion.2 = bf16[2048,4096]{1,0:T(8,128)(2,1)} fusion(bf16[2048,8192]{1,0:T(8,128)(2,1)} %all-gather.16.cloned.1.call-done, s32[]{:T(128)S(6)} %select_n.132), kind=kLoop, calls=%fused_computation.85 | loop fusion | bytes 33554436 | tf_op jit(solution)/shard_map/dynamic_slice | solution.py:196
  1264.7 16.8 %constant_dynamic-slice_fusion.1 = bf16[2048,4096]{1,0:T(8,128)(2,1)} fusion(bf16[2048,8192]{1,0:T(8,128)(2,1)} %all-gather.18.cloned.1.call-done, s32[]{:T(128)S(6)} %select_n.132), kind=kLoop, calls=%fused_computation.84 | loop fusion | bytes 33554436 | tf_op jit(solution)/shard_map/dynamic_slice | solution.py:196
  1281.5 6.6 constant_dynamic-slice_fusion
  1288.1 45.0 %collective-permute-done.3 = bf16[2,512,2048]{2,1,0:T(8,128)(2,1)S(1)} collective-permute-done((bf16[2,512,2048]{2,1,0:T(8,128)(2,1)}, bf16[2,512,2048]{2,1,0:T(8,128)(2,1)S(1)}, u32[]{:S(2)}, u32[]{:S(2)}) %collective-permute-start.3) | collective-permute-done | bytes 4194336 | tf_op jit(solution)/shard_map/ppermute | solution.py:236
  1333.1 2.3 constant_dynamic-update-slice_fusion
  (47 shorter events, 0.2 us)
Async XLA Ops:
  7.2 1.9 copy-start
  7.2 57.9 %all-gather.10.cloned.1.call-start = ((), (), s32[]{:S(2)}) async-start(), calls=%async_computation.1 | async-start | bytes 9437184 | tf_op jit(solution)/shard_map/all_gather | solution.py:197
  13.7 10.8 copy-start.5
  13.7 11.4 copy-start.6
  13.7 102.1 %all-gather.12.cloned.1.call-start = ((), (), s32[]{:S(2)}) async-start(), calls=%async_computation.2 | async-start | bytes 9437184 | tf_op jit(solution)/shard_map/all_gather | solution.py:197
  14.5 152.1 %all-gather.8.cloned.1.call-start = ((), (), s32[]{:S(2)}) async-start(), calls=%async_computation | async-start | bytes 9437184 | tf_op jit(solution)/shard_map/all_gather | solution.py:197
  15.2 384.7 %all-gather.14.cloned.1.call-start = ((), (), s32[]{:S(2)}) async-start(), calls=%async_computation.3 | async-start | bytes 9437184 | tf_op jit(solution)/shard_map/all_gather | solution.py:198
  15.8 428.2 %all-gather.16.cloned.1.call-start = ((), (), s32[]{:S(2)}) async-start(), calls=%async_computation.4 | async-start | bytes 37748736 | tf_op jit(solution)/shard_map/all_gather | solution.py:197
  21.9 577.0 %all-gather.18.cloned.1.call-start = ((), (), s32[]{:S(2)}) async-start(), calls=%async_computation.5 | async-start | bytes 37748736 | tf_op jit(solution)/shard_map/all_gather | solution.py:197
  22.5 737.1 %all-gather.20.cloned.1.call-start = ((), (), s32[]{:S(2)}) async-start(), calls=%async_computation.6 | async-start | bytes 37748736 | tf_op jit(solution)/shard_map/all_gather | solution.py:198
  25.2 13.1 copy-start.7
  399.9 44.0 %copy-start.4 = (f32[2048]{0:T(1024)S(1)}, f32[2048]{0:T(1024)}, u32[]{:S(2)}) copy-start(f32[2048]{0:T(1024)} %convert_element_type.109) | copy-start | bytes 24580
  816.0 92.7 %collective-permute-start = (bf16[2,512,2048]{2,1,0:T(8,128)(2,1)}, bf16[2,512,2048]{2,1,0:T(8,128)(2,1)}, u32[]{:S(2)}, u32[]{:S(2)}) collective-permute-start(bf16[2,512,2048]{2,1,0:T(8,128)(2,1)} %get-tuple-element.47), channel_id=1, source_target_pairs={{0,4},{4,0},{1,5},{5,1},{2,6},{6,2},{3,7},{7,3}} | collective-permute-start | bytes 12582920 | tf_op jit(solution)/shard_map/ppermute | solution.py:236
  958.6 92.0 %collective-permute-start.1 = (bf16[2,512,2048]{2,1,0:T(8,128)(2,1)}, bf16[2,512,2048]{2,1,0:T(8,128)(2,1)}, u32[]{:S(2)}, u32[]{:S(2)}) collective-permute-start(bf16[2,512,2048]{2,1,0:T(8,128)(2,1)} %get-tuple-element.49), channel_id=1, source_target_pairs={{0,4},{4,0},{1,5},{5,1},{2,6},{6,2},{3,7},{7,3}} | collective-permute-start | bytes 12582920 | tf_op jit(solution)/shard_map/ppermute | solution.py:236
  963.1 138.7 %copy-start.2 = (bf16[2048,1024]{0,1:T(8,128)(2,1)}, bf16[2048,1024]{0,1:T(8,128)(2,1)S(1)}, u32[]{:S(2)}) copy-start(bf16[2048,1024]{0,1:T(8,128)(2,1)S(1)} %constant_dynamic-slice_fusion.6) | copy-start | bytes 12582916
  967.1 23.6 %copy-start.3 = (bf16[2048,1024]{0,1:T(8,128)(2,1)}, bf16[2048,1024]{0,1:T(8,128)(2,1)S(1)}, u32[]{:S(2)}) copy-start(bf16[2048,1024]{0,1:T(8,128)(2,1)S(1)} %constant_dynamic-slice_fusion.5) | copy-start | bytes 12582916
  1100.4 92.0 %collective-permute-start.2 = (bf16[2,512,2048]{2,1,0:T(8,128)(2,1)}, bf16[2,512,2048]{2,1,0:T(8,128)(2,1)}, u32[]{:S(2)}, u32[]{:S(2)}) collective-permute-start(bf16[2,512,2048]{2,1,0:T(8,128)(2,1)} %get-tuple-element.51), channel_id=1, source_target_pairs={{0,4},{4,0},{1,5},{5,1},{2,6},{6,2},{3,7},{7,3}} | collective-permute-start | bytes 12582920 | tf_op jit(solution)/shard_map/ppermute | solution.py:236
  1242.2 90.9 %collective-permute-start.3 = (bf16[2,512,2048]{2,1,0:T(8,128)(2,1)}, bf16[2,512,2048]{2,1,0:T(8,128)(2,1)S(1)}, u32[]{:S(2)}, u32[]{:S(2)}) collective-permute-start(bf16[2,512,2048]{2,1,0:T(8,128)(2,1)} %get-tuple-element.53), channel_id=1, source_target_pairs={{0,4},{4,0},{1,5},{5,1},{2,6},{6,2},{3,7},{7,3}} | collective-permute-start | bytes 12582920 | tf_op jit(solution)/shard_map/ppermute | solution.py:236
  1247.7 33.8 %slice-start = ((s8[33554432]{0:T(1024)(128)(4,1)}), s8[4194304]{0:T(1024)(128)(4,1)S(1)}, s32[]{:S(2)}) async-start(s8[33554432]{0:T(1024)(128)(4,1)} %bitcast.82), calls=%async_computation.7 | async-start | bytes 8388608
  1247.7 33.8 %slice-start.1 = ((s8[33554432]{0:T(1024)(128)(4,1)}), s8[4194304]{0:T(1024)(128)(4,1)S(1)}, s32[]{:S(2)}) async-start(s8[33554432]{0:T(1024)(128)(4,1)} %bitcast.82), calls=%async_computation.8 | async-start | bytes 8388608
  1247.7 33.8 %slice-start.2 = ((s8[33554432]{0:T(1024)(128)(4,1)}), s8[4194304]{0:T(1024)(128)(4,1)S(1)}, s32[]{:S(2)}) async-start(s8[33554432]{0:T(1024)(128)(4,1)} %bitcast.82), calls=%async_computation.9 | async-start | bytes 8388608
  1247.7 33.8 %slice-start.3 = ((s8[33554432]{0:T(1024)(128)(4,1)}), s8[4194304]{0:T(1024)(128)(4,1)S(1)}, s32[]{:S(2)}) async-start(s8[33554432]{0:T(1024)(128)(4,1)} %bitcast.82), calls=%async_computation.10 | async-start | bytes 8388608
  1264.6 16.9 %slice-start.4 = ((s8[33554432]{0:T(1024)(128)(4,1)}), s8[4194304]{0:T(1024)(128)(4,1)S(1)}, s32[]{:S(2)}) async-start(s8[33554432]{0:T(1024)(128)(4,1)} %bitcast.82), calls=%async_computation.11 | async-start | bytes 8388608
  1264.6 16.9 %slice-start.5 = ((s8[33554432]{0:T(1024)(128)(4,1)}), s8[4194304]{0:T(1024)(128)(4,1)S(1)}, s32[]{:S(2)}) async-start(s8[33554432]{0:T(1024)(128)(4,1)} %bitcast.82), calls=%async_computation.12 | async-start | bytes 8388608
  1264.6 16.9 %slice-start.6 = ((s8[33554432]{0:T(1024)(128)(4,1)}), s8[4194304]{0:T(1024)(128)(4,1)S(1)}, s32[]{:S(2)}) async-start(s8[33554432]{0:T(1024)(128)(4,1)} %bitcast.82), calls=%async_computation.13 | async-start | bytes 8388608
  1264.6 16.9 %slice-start.7 = ((s8[33554432]{0:T(1024)(128)(4,1)}), s8[4194304]{0:T(1024)(128)(4,1)S(1)}, s32[]{:S(2)}) async-start(s8[33554432]{0:T(1024)(128)(4,1)} %bitcast.82), calls=%async_computation.14 | async-start | bytes 8388608
  1264.6 70.8 %copy-start.1 = (bf16[2048,768]{1,0:T(8,128)(2,1)S(1)}, bf16[2048,768]{1,0:T(8,128)(2,1)}, u32[]{:S(2)}) copy-start(bf16[2048,768]{1,0:T(8,128)(2,1)} %param.14) | copy-start | bytes 9437188
Sparse Core Ops, SparseCore 0:
  13.9 51.1 all-gather.9
  67.5 48.3 all-gather.11
  118.2 48.3 all-gather.7
  168.3 48.3 all-gather.13
  218.9 155.2 all-gather.15
  376.4 155.2 all-gather.17
  533.5 155.2 all-gather.19

commit v2 on v1

--- a/solution.py
+++ b/solution.py
@@ -7,6 +7,7 @@
 from jax.experimental.layout import Layout, with_layout_constraint
 from jax.experimental.pallas import tpu as pltpu
 from jax.sharding import PartitionSpec as P
+
 
 ROPE_BASE = 500000.0
 ROPE_FACTOR = 8.0
@@ -18,7 +19,7 @@
 BF16 = jnp.bfloat16
 F32 = jnp.float32
 SHARED = 0
-CHUNK = 2
+CHUNKS = (1, 1, 2, 2, 2)
 
 
 def rms_norm(x_in, gain_vec):
@@ -53,32 +54,45 @@
 def attn_kernel(len_ref, q_ref, k_ref, v_ref, cos_ref, sin_ref, cos_t_ref, sin_t_ref, o_ref, *, half, blk):
     seq = q_ref.shape[1]
     hd = 2 * half
+    pair = 2 * hd
     length = len_ref[pl.program_id(0)]
     cos_t, sin_t = cos_t_ref[...], sin_t_ref[...]
-    keys = []
-    for h in range(2):
-        k_first = k_ref[0, h * hd:h * hd + half, :].astype(F32)
-        k_second = k_ref[0, h * hd + half:(h + 1) * hd, :].astype(F32)
-        lo, hi = rope_rows(k_first, k_second, cos_t, sin_t)
-        keys.append(jnp.concatenate([lo, hi], axis=0).astype(BF16))
-    for i in range(seq // blk):
-        rows = slice(i * blk, (i + 1) * blk)
-        width = (i + 1) * blk
-        q_in = q_ref[0, rows, :].astype(F32)
-        lane = lax.broadcasted_iota(jnp.int32, q_in.shape, 1)
-        swapped = jnp.where(lane % hd < half, pltpu.roll(q_in, 2 * hd - half, 1), pltpu.roll(q_in, half, 1))
-        q_rot = (q_in * cos_ref[rows, :] + swapped * sin_ref[rows, :]).astype(BF16) * BF16(hd ** -0.5)
-        row = lax.broadcasted_iota(jnp.int32, (blk, width), 0) + i * blk
-        col = lax.broadcasted_iota(jnp.int32, (blk, width), 1)
-        allowed = col <= jnp.minimum(row, length - 1)
-        outs = []
+    lane = lax.broadcasted_iota(jnp.int32, (blk, pair), 1)
+    blocks = range(seq // blk)
+    masks = []
+    for i in blocks:
+        row = lax.broadcasted_iota(jnp.int32, (blk, (i + 1) * blk), 0) + i * blk
+        col = lax.broadcasted_iota(jnp.int32, (blk, (i + 1) * blk), 1)
+        masks.append(col <= jnp.minimum(row, length - 1))
+    for p in range(q_ref.shape[2] // pair):
+        cols = slice(p * pair, (p + 1) * pair)
+        keys = []
         for h in range(2):
-            scores = jnp.dot(q_rot[:, h * hd:(h + 1) * hd], keys[h][:, :width], preferred_element_type=F32)
-            scores = jnp.where(allowed, scores, MASK_VALUE)
-            expd = jnp.exp(scores - jnp.max(scores, axis=-1, keepdims=True))
-            prob = (expd * (1.0 / jnp.sum(expd, axis=-1, keepdims=True))).astype(BF16)
-            outs.append(lax.dot_general(prob, v_ref[0, :, :width], (((1,), (1,)), ((), ())), preferred_element_type=F32))
-        o_ref[0, rows, :] = jnp.where(lane < hd, outs[0], outs[1]).astype(BF16)
+            at = p * pair + h * hd
+            keys += rope_rows(k_ref[0, at:at + half, :].astype(F32), k_ref[0, at + half:at + hd, :].astype(F32), cos_t, sin_t)
+        keys = jnp.concatenate([part.astype(BF16) for part in keys], axis=0)
+        scores = {}
+        for i in blocks:
+            rows = slice(i * blk, (i + 1) * blk)
+            q_in = q_ref[0, rows, cols].astype(F32)
+            swapped = jnp.where(lane % hd < half, pltpu.roll(q_in, pair - half, 1), pltpu.roll(q_in, half, 1))
+            q_rot = (q_in * cos_ref[rows, :] + swapped * sin_ref[rows, :]).astype(BF16) * BF16(hd ** -0.5)
+            for h in range(2):
+                q_head = jnp.where(lane // hd == h, q_rot, BF16(0))
+                scores[i, h] = jnp.dot(q_head, keys[:, :(i + 1) * blk], preferred_element_type=F32)
+        tops = {}
+        for i, h in scores:
+            scores[i, h] = jnp.where(masks[i], scores[i, h], MASK_VALUE)
+            tops[i, h] = jnp.max(scores[i, h], axis=-1, keepdims=True)
+        values = v_ref[0, cols, :]
+        outs = {}
+        for i, h in scores:
+            expd = jnp.exp(scores[i, h] - tops[i, h])
+            norm = 1.0 / jnp.sum(expd, axis=-1, keepdims=True)
+            out = lax.dot_general(expd.astype(BF16), values[:, :(i + 1) * blk], (((1,), (1,)), ((), ())), preferred_element_type=F32)
+            outs[i, h] = out * norm
+        for i in blocks:
+            o_ref[0, i * blk:(i + 1) * blk, cols] = jnp.where(lane < hd, outs[i, 0], outs[i, 1]).astype(BF16)
 
 
 def attention(lengths, q, k_t, v_t, angles):
@@ -89,18 +103,19 @@
     cos_row = jnp.tile(jnp.concatenate([cos, cos], axis=1), (1, 2))
     sin_row = jnp.tile(jnp.concatenate([-sin, sin], axis=1), (1, 2))
     whole = lambda shape: pl.BlockSpec(shape, lambda b, j, *_: (0, 0))
+    group = 4 * hd
     return pl.pallas_call(
         functools.partial(attn_kernel, half=half, blk=256),
         grid_spec=pltpu.PrefetchScalarGridSpec(
             num_scalar_prefetch=1,
-            grid=(batch, width // (2 * hd)),
+            grid=(batch, width // group),
             in_specs=[
-                pl.BlockSpec((1, seq, 2 * hd), lambda b, j, *_: (b, 0, j)),
-                pl.BlockSpec((1, 2 * hd, seq), lambda b, j, *_: (b, j, 0)),
-                pl.BlockSpec((1, 2 * hd, seq), lambda b, j, *_: (b, j, 0)),
+                pl.BlockSpec((1, seq, group), lambda b, j, *_: (b, 0, j)),
+                pl.BlockSpec((1, group, seq), lambda b, j, *_: (b, j, 0)),
+                pl.BlockSpec((1, group, seq), lambda b, j, *_: (b, j, 0)),
                 whole((seq, 2 * hd)), whole((seq, 2 * hd)), whole((half, seq)), whole((half, seq)),
             ],
-            out_specs=pl.BlockSpec((1, seq, 2 * hd), lambda b, j, *_: (b, 0, j)),
+            out_specs=pl.BlockSpec((1, seq, group), lambda b, j, *_: (b, 0, j)),
         ),
         out_shape=jax.ShapeDtypeStruct(q.shape, BF16),
         compiler_params=pltpu.CompilerParams(dimension_semantics=("parallel", "arbitrary")),
@@ -179,7 +194,7 @@
     source = (rest // head_dim) * 3 * head_dim + kind * head_dim + rest % head_dim
     select = (jnp.arange(cols)[:, None] == source[None, :]).astype(BF16)
     plain = jnp.dot(w_qkv, select, preferred_element_type=F32).astype(BF16)
-    return plain[:, :third], plain[:, third:2 * third], plain[:, 2 * third:]
+    return [with_layout_constraint(plain[:, k * third:(k + 1) * third], Layout((0, 1))) for k in range(3)]
 
 
 def solution(mesh):
@@ -187,21 +202,24 @@
 
     def local_step(x_loc, len_loc, k_buf, v_buf, w_qkv, w_o, w_gate_up, w_down, g_attn, g_mlp):
         batch, seq, _ = x_loc.shape
-        heads, head_dim = k_buf.shape[2:]
+        _, head_dim = k_buf.shape[2:]
         n_oth = batch // n_tpa - SHARED // 2
         n_own = batch - n_oth
         mine = lax.axis_index('tpa')
         own_at, oth_at = mine * n_oth, (1 - mine) * n_own
         axes = ('tpa', 'tpb')
         take = lambda arr, at, n, axis=0: lax.dynamic_slice_in_dim(arr, at, n, axis)
-        cols = lambda w: lax.all_gather(w, axes, axis=1, tiled=True)
+        cols = lambda w: with_layout_constraint(lax.all_gather(w, axes, axis=1, tiled=True), Layout((0, 1)))
         rows = lambda w: lax.all_gather(w, axes, axis=0, tiled=True)
 
         wq, wk, wv = unpack_qkv(w_qkv, head_dim)
         ff = w_gate_up.shape[1] // 2
-        wk, wv, wq = cols(wk), cols(wv), cols(wq)
+        wk = cols(wk)
+        wv = cols(wv)
+        wq = cols(wq)
         wo = rows(w_o)
-        wgate, wup = cols(w_gate_up[:, :ff]), cols(w_gate_up[:, ff:])
+        wgate = cols(w_gate_up[:, :ff])
+        wup = cols(w_gate_up[:, ff:])
         wdown = rows(w_down)
         share = lambda w, axis: take(w, mine * (w.shape[axis] // n_tpa), w.shape[axis] // n_tpa, axis)
         out_w = (share(wq, 1), share(wk, 1), share(wv, 1), share(wo, 0), share(wgate, 1), share(wup, 1), share(wdown, 0))
@@ -212,7 +230,8 @@
         len_own = take(len_loc, own_at, n_own)
         k_t, v_t = matmul_t(u_own, wk), matmul_t(u_own, wv)
         q = matmul(u_own, wq).astype(BF16)
-        k_oth, v_oth = matmul_t(u_oth, out_w[1]), matmul_t(u_oth, out_w[2])
+        k_oth = matmul_t(u_oth, out_w[1])
+        v_oth = matmul_t(u_oth, out_w[2])
         attn = attention(len_own, q, k_t, v_t, angles)
         hidden = (x_own.astype(F32) + matmul(attn, wo)).astype(BF16)
         u2 = rms_norm(hidden, g_mlp)
@@ -227,15 +246,21 @@
         back = lambda t: jnp.transpose(t, (0, 3, 1, 2))
 
         swap = [(i, n_tpa - 1 - i) for i in range(n_tpa)]
-        y_out = jnp.zeros(x_loc.shape, BF16)
         sent_at = mine * (n_own - n_oth)
-        for start in range(0, n_oth, CHUNK):
-            n = min(CHUNK, n_oth - start)
-            local = sent_at + start
+        parts = []
+        at = 0
+        for n in CHUNKS:
+            local = sent_at + at
             part = (take(hidden, local, n).astype(F32) + matmul(take(mid, local, n), wdown)).astype(BF16)
             other = lax.ppermute(part, 'tpa', swap)
+            parts.append((at, local, part, other))
+            at += n
+        assert at == n_oth
+        y_out = jnp.zeros(x_loc.shape, BF16)
+        for at, local, part, _ in parts:
             y_out = lax.dynamic_update_slice_in_dim(y_out, part, own_at + local, 0)
-            y_out = lax.dynamic_update_slice_in_dim(y_out, other, oth_at + start, 0)
+        for at, local, _, other in parts:
+            y_out = lax.dynamic_update_slice_in_dim(y_out, other, oth_at + at, 0)
         return (y_out, back(k_cache), back(v_cache)) + out_w
 
     batch_spec = P(('part', 'tpb'), None, None)
@@ -246,4 +271,5 @@
     gain_spec = P('part')
     gen_cols = P('part', 'tpa')
     gen_rows = P(('part', 'tpa'), None)
+
     return jax.shard_map(local_step, mesh=mesh, in_specs=(batch_spec, len_spec, cache_spec, cache_spec, train_cols, train_rows, train_cols, train_rows, gain_spec, gain_spec), out_specs=(batch_spec, cache_spec, cache_spec, gen_cols, gen_cols, gen_cols, gen_rows, gen_cols, gen_cols, gen_rows), check_vma=False)

time: 1350 us -> 1290 us (0.956)
  Pallas kernels: 236 us -> 149 us
  waiting for transfers between devices: 219 us -> 255 us
  local copies, waits for them, and re-layouts: 115 us -> 101 us
    pallas_call x1, Pallas kernels: 191 us -> 103 us  [attention(): pl.pallas_call(functools.partial(attn_kernel, half=half, blk=256), grid_s...]
    ppermute x4 -> x5, waiting for transfers between devices: 196 us -> 223 us  [local_step(): other = lax.ppermute(part, 'tpa', swap)]
    unnamed x35 -> x36, local copies, waits for them, and re-layouts: 21.1 us -> 5.9 us
    dot_general x12 -> x13, matrix products: 712 us -> 716 us  [matmul(): return jnp.einsum('bsd,dc->bsc', lhs, rhs, preferred_element_type=F32)]
  transfers between devices with their start and end apart: 11 -> 12, of which waited for: 6 -> 3; matrix products, arithmetic and copies ran while one was open for 49% -> 61% of each run, Pallas kernels for 18% -> 12%
where the time goes in v2:
time: 1290 us; the launch traced here: 1280 us
  matrix products  719 us (56%)
  waiting for transfers between devices  255 us (20%)
  Pallas kernels  149 us (12%)
  local copies, waits for them, and re-layouts  101 us (8%)
  other arithmetic  38 us (3%)
  between operations  14.6 us (1%)
    dot_general x13, matrix products, matmul(): return jnp.einsum('bsd,dc->bsc', lhs, rhs, preferred_element_type=F32)  716 us
    ppermute x5, waiting for transfers between devices, local_step(): other = lax.ppermute(part, 'tpa', swap)  223 us
    pallas_call x1, Pallas kernels, attention(): pl.pallas_call(functools.partial(attn_kernel, half=half, blk=256), grid_s...  103 us
    dynamic_slice x8, local copies, waits for them, and re-layouts, local_step(): take = lambda arr, at, n, axis=0: lax.dynamic_slice_in_dim(arr, at, n, axis)  56.1 us
    pallas_call x1, Pallas kernels, fill_cache(): pl.pallas_call(functools.partial(cache_kernel, n_own=n_own), grid_spec=pl...  45.9 us
    all_gather x5, waiting for transfers between devices, local_step(): lax.all_gather(w, axes, axis=1, tiled=True)  28.7 us
  transfers between devices with their start and end apart: 12, of which 3 were waited for; matrix products, arithmetic and copies ran while one was open for 61% of the time, Pallas kernels for 12%

profile of v2, /device:TPU:0, one launch (start us, length us, event | category | flops | bytes accessed | tf_op | source)
XLA Modules:
  0.0 1281.3 jit_solution(3055996872588000288)
XLA Ops:
  7.2 0.0 all-gather.12.cloned.1.call-start
  7.3 1.8 copy-done
  9.1 2.9 fusion.51
  12.0 1.7 fusion.82
  13.8 0.0 all-gather.10.cloned.1.call-start
  13.8 0.7 all-gather.10.cloned.1.call-update
  14.5 0.0 all-gather.8.cloned.1.call-start
  14.5 0.7 all-gather.8.cloned.1.call-update
  15.2 0.0 all-gather.14.cloned.1.call-start
  15.3 0.5 all-gather.14.cloned.1.call-update
  15.8 0.0 all-gather.16.cloned.1.call-start
  15.9 6.3 fusion.81
  22.1 0.0 all-gather.16.cloned.1.call-update
  22.1 0.0 all-gather.18.cloned.1.call-start
  22.2 0.5 all-gather.18.cloned.1.call-update
  22.7 0.0 all-gather.20.cloned.1.call-start
  22.8 0.7 all-gather.20.cloned.1.call-update
  23.5 1.0 fusion.53
  24.5 0.3 fusion.57
  24.8 0.6 convert_element_type.115
  25.4 11.9 fusion.5
  37.3 0.8 copy.24.cos_ref
  38.2 0.9 copy.25.sin_ref
  39.1 0.5 dynamic_slice.64.len_ref
  39.6 23.6 %fusion.7 = bf16[16,512,2048]{2,1,0:T(8,128)(2,1)} fusion(bf16[16,512,2048]{2,1,0:T(8,128)(2,1)} %param.10, f32[2048]{0:T(1024)S(1)} %convert_element_type.103, f32[16,512]{1,0:T(8,128)S(1)} %add_rsqrt_fusion), kind=kLoop, calls=%fused_computation.11 | loop fusion | flops 67108864 | bytes 67149824 | tf_op jit(solution)/shard_map/convert_element_type | solution.py:28
  63.2 0.6 pad_add_fusion.pos_ref
  63.8 3.2 all-gather.12.cloned.1.call-done
  67.0 2.6 constant_dynamic-slice_fusion.5
  69.7 2.0 copy-done.2
  71.7 22.7 %fusion.38 = bf16[8,512,1024]{1,2,0:T(8,128)(2,1)} fusion(bf16[16,512,2048]{2,1,0:T(8,128)(2,1)} %fusion.7, s32[]{:T(128)S(6)} %select_n.134, bf16[2048,1024]{1,0:T(8,128)(2,1)S(1)} %constant_dynamic-slice_fusion.5), kind=kOutput, calls=%fused_computation.49 | convolution fusion | flops 17184063488 | bytes 29360132 | tf_op jit(solution)/shard_map/bsd,dc->bsc/dot_general | solution.py:42
  94.4 25.4 %all-gather.10.cloned.1.call-done = bf16[2048,2048]{1,0:T(8,128)(2,1)} async-done(((bf16[2048,256]{1,0:T(8,128)(2,1)}), bf16[2048,2048]{1,0:T(8,128)(2,1)}) %all-gather.10.cloned.1.call-update) | async-done | bytes 8388624 | tf_op jit(solution)/shard_map/all_gather | solution.py:212
  119.8 2.6 constant_dynamic-slice_fusion.6
  122.5 2.0 copy-done.3
  124.5 22.9 %fusion.35 = bf16[8,512,1024]{1,2,0:T(8,128)(2,1)} fusion(bf16[16,512,2048]{2,1,0:T(8,128)(2,1)} %fusion.7, s32[]{:T(128)S(6)} %select_n.134, bf16[2048,1024]{1,0:T(8,128)(2,1)S(1)} %constant_dynamic-slice_fusion.6), kind=kOutput, calls=%fused_computation.48 | convolution fusion | flops 17184063488 | bytes 29360132 | tf_op jit(solution)/shard_map/bsd,dc->bsc/dot_general | solution.py:42
  147.4 42.4 %convolution_convert_fusion.1 = bf16[8,512,2048]{1,2,0:T(8,128)(2,1)} fusion(bf16[16,512,2048]{2,1,0:T(8,128)(2,1)} %fusion.7, s32[]{:T(128)S(6)} %select_n.123, bf16[2048,2048]{1,0:T(8,128)(2,1)} %all-gather.10.cloned.1.call-done), kind=kOutput, calls=%fused_computation.32 | convolution fusion | flops 34368126976 | bytes 41943044 | tf_op jit(solution)/shard_map/bsd,dc->bsc/dot_general | solution.py:42
  189.8 39.5 %convolution_convert_fusion = bf16[8,512,2048]{1,2,0:T(8,128)(2,1)} fusion(bf16[16,512,2048]{2,1,0:T(8,128)(2,1)} %fusion.7, s32[]{:T(128)S(6)} %select_n.123, bf16[2048,2048]{1,0:T(8,128)(2,1)S(1)} %bitcast.102), kind=kOutput, calls=%fused_computation.31 | convolution fusion | flops 34368126976 | bytes 41943044 | tf_op jit(solution)/shard_map/bsd,dc->bsc/dot_general | solution.py:42
  229.2 43.6 %convolution_convert_fusion.2.q_ref = bf16[8,512,2048]{2,1,0:T(8,128)(2,1)} fusion(bf16[16,512,2048]{2,1,0:T(8,128)(2,1)} %fusion.7, s32[]{:T(128)S(6)} %select_n.123, bf16[2048,2048]{1,0:T(8,128)(2,1)} %all-gather.8.cloned.1.call-done), kind=kOutput, calls=%fused_computation.33 | convolution fusion | flops 34368126976 | bytes 41943044 | tf_op jit(solution)/shard_map/bsd,dc->bsc/dot_general | solution.py:42
  272.8 103.2 %prefill_attention.1 = bf16[8,512,2048]{2,1,0:T(8,128)(2,1)} custom-call(s32[8]{0:T(128)} %dynamic_slice.64.len_ref, bf16[8,512,2048]{2,1,0:T(8,128)(2,1)} %convolution_convert_fusion.2.q_ref, bf16[8,2048,512]{2,1,0:T(8,128)(2,1)} %bitcast.109, bf16[8,2048,512]{2,1,0:T(8,128)(2,1)} %bitcast.111, f32[512,128]{1,0:T(8,128)} %copy.24.cos_ref, ...), custom_call_target="tpu_custom_call" | custom-call | flops 68719476736 | bytes 67108864 | tf_op jit(solution)/shard_map/prefill_attention/pallas_call | solution.py:107
  376.0 44.5 %fusion.8 = (f32[8,512]{1,0:T(8,128)S(1)}, bf16[8,512,2048]{2,1,0:T(8,128)(2,1)}) fusion(bf16[8,512,2048]{2,1,0:T(8,128)(2,1)} %prefill_attention.1, bf16[2048,2048]{1,0:T(8,128)(2,1)} %all-gather.14.cloned.1.call-done, bf16[16,512,2048]{2,1,0:T(8,128)(2,1)} %param.10, s32[]{:T(128)S(6)} %select_n.123), kind=kOutput, calls=%fused_computation.14 | convolution fusion | flops 34410065920 | bytes 58736644 | tf_op jit(solution)/shard_map/bsd,dc->bsc/dot_general | solution.py:42
  420.5 45.9 %fill_cache.1 = (bf16[16,16,64,512]{3,2,1,0:T(8,128)(2,1)}, bf16[16,16,64,512]{3,2,1,0:T(8,128)(2,1)}) custom-call(s32[3]{0:T(128)} %pad_add_fusion.pos_ref, s32[16]{0:T(128)} %len_ref.1, bf16[8,32,64,512]{3,2,1,0:T(8,128)(2,1)} %bitcast.110, bf16[8,32,64,512]{3,2,1,0:T(8,128)(2,1)} %bitcast.112, bf16[8,16,64,512]{3,2,1,0:T(8,128)(2,1)} %bitcast.114, ...), custom_call_target="tpu_custom_call" | custom-call | flops 40000000000 | bytes 100663296 | tf_op jit(solution)/shard_map/fill_cache/pallas_call | solution.py:174
  466.5 5.0 constant_dynamic-slice_fusion.4
  471.5 4.8 constant_dynamic-slice_fusion.3
  476.3 154.9 %fusion.18 = bf16[8,512,8192]{2,1,0:T(8,128)(2,1)} fusion(bf16[2048,8192]{1,0:T(8,128)(2,1)} %all-gather.16.cloned.1.call-done, bf16[8,512,2048]{2,1,0:T(8,128)(2,1)} %get-tuple-element.25, f32[2048]{0:T(1024)S(1)} %copy-done.4, f32[8,512]{1,0:T(8,128)S(1)} %add_rsqrt_fusion.1), kind=kOutput, calls=%fused_computation.24 | convolution fusion | flops 137472507904 | bytes 117465088 | tf_op jit(solution)/shard_map/bsd,dc->bsc/dot_general | solution.py:42
  631.1 160.6 %fusion.4 = bf16[8,512,8192]{2,1,0:T(8,128)(2,1)} fusion(bf16[8,512,8192]{2,1,0:T(8,128)(2,1)} %fusion.18, bf16[2048,8192]{1,0:T(8,128)(2,1)} %all-gather.18.cloned.1.call-done, bf16[8,512,2048]{2,1,0:T(8,128)(2,1)} %get-tuple-element.25, f32[2048]{0:T(1024)S(1)} %copy-done.4, f32[8,512]{1,0:T(8,128)S(1)} %add_rsqrt_fusion.1), kind=kOutput, calls=%fused_computation.6 | convolution fusion | flops 137774497792 | bytes 184573952 | tf_op jit(solution)/shard_map/bsd,dc->bsc/dot_general | solution.py:42
  791.8 11.2 broadcast_in_dim.2
  802.9 24.9 %constant_dynamic-update-slice_fusion.9 = (bf16[16,512,2048]{2,1,0:T(8,128)(2,1)}, bf16[1,512,2048]{2,1,0:T(8,128)(2,1)}) fusion(bf16[16,512,2048]{2,1,0:T(8,128)(2,1)} %broadcast_in_dim.2, s32[]{:T(128)S(6)} %select_n.123, bf16[8192,2048]{1,0:T(8,128)(2,1)} %all-gather.20.cloned.1.call-done, bf16[8,512,8192]{2,1,0:T(8,128)(2,1)} %fusion.4, ...), kind=kOutput, calls=%fused_computation.104 | convolution fusion | flops 17183014912 | bytes 48234500 | tf_op jit(solution)/shard_map/bsd,dc->bsc/dot_general | solution.py:42
  827.8 25.2 %constant_dynamic-update-slice_fusion.8 = (bf16[16,512,2048]{2,1,0:T(8,128)(2,1)}, bf16[1,512,2048]{2,1,0:T(8,128)(2,1)}) fusion(bf16[16,512,2048]{2,1,0:T(8,128)(2,1)} %get-tuple-element.26, s32[]{:T(128)S(6)} %select_n.130, bf16[8192,2048]{1,0:T(8,128)(2,1)} %all-gather.20.cloned.1.call-done, bf16[8,512,8192]{2,1,0:T(8,128)(2,1)} %fusion.4, ...), kind=kOutput, calls=%fused_computation.103 | convolution fusion | flops 17183014912 | bytes 48234500 | tf_op jit(solution)/shard_map/bsd,dc->bsc/dot_general | solution.py:42
  853.0 0.1 collective-permute-start.1
  853.1 2.0 collective-permute-start
  855.0 45.1 %constant_dynamic-update-slice_fusion.7 = (bf16[16,512,2048]{2,1,0:T(8,128)(2,1)}, bf16[2,512,2048]{2,1,0:T(8,128)(2,1)}) fusion(bf16[16,512,2048]{2,1,0:T(8,128)(2,1)} %get-tuple-element.28, s32[]{:T(128)S(6)} %select_n.131, bf16[8,512,8192]{2,1,0:T(8,128)(2,1)} %fusion.4, bf16[8192,2048]{1,0:T(8,128)(2,1)} %all-gather.20.cloned.1.call-done, ...), kind=kOutput, calls=%fused_computation.102 | convolution fusion | flops 34366029824 | bytes 113246208 | tf_op jit(solution)/shard_map/bsd,dc->bsc/dot_general | solution.py:42
  900.1 45.3 %constant_dynamic-update-slice_fusion.6 = (bf16[16,512,2048]{2,1,0:T(8,128)(2,1)}, bf16[2,512,2048]{2,1,0:T(8,128)(2,1)}) fusion(bf16[16,512,2048]{2,1,0:T(8,128)(2,1)} %get-tuple-element.30, s32[]{:T(128)S(6)} %select_n.132, bf16[8,512,8192]{2,1,0:T(8,128)(2,1)} %fusion.4, bf16[8192,2048]{1,0:T(8,128)(2,1)} %all-gather.20.cloned.1.call-done, ...), kind=kOutput, calls=%fused_computation.101 | convolution fusion | flops 34366029824 | bytes 113246208 | tf_op jit(solution)/shard_map/bsd,dc->bsc/dot_general | solution.py:42
  945.4 45.1 %constant_dynamic-update-slice_fusion.5 = (bf16[16,512,2048]{2,1,0:T(8,128)(2,1)}, bf16[2,512,2048]{2,1,0:T(8,128)(2,1)}) fusion(bf16[16,512,2048]{2,1,0:T(8,128)(2,1)} %get-tuple-element.32, s32[]{:T(128)S(6)} %select_n.133, bf16[8,512,8192]{2,1,0:T(8,128)(2,1)} %fusion.4, bf16[8192,2048]{1,0:T(8,128)(2,1)} %all-gather.20.cloned.1.call-done, ...), kind=kOutput, calls=%fused_computation.100 | convolution fusion | flops 34366029824 | bytes 113246208 | tf_op jit(solution)/shard_map/bsd,dc->bsc/dot_general | solution.py:42
  990.5 0.1 collective-permute-start.4
  990.5 2.0 collective-permute-start.3
  992.5 0.1 collective-permute-start.2
  992.6 17.0 %constant_dynamic-slice_fusion.2 = bf16[2048,4096]{1,0:T(8,128)(2,1)} fusion(bf16[2048,8192]{1,0:T(8,128)(2,1)} %all-gather.16.cloned.1.call-done, s32[]{:T(128)S(6)} %select_n.140), kind=kLoop, calls=%fused_computation.89 | loop fusion | bytes 33554436 | tf_op jit(solution)/shard_map/dynamic_slice | solution.py:211
  1009.6 17.0 %constant_dynamic-slice_fusion.1 = bf16[2048,4096]{1,0:T(8,128)(2,1)} fusion(bf16[2048,8192]{1,0:T(8,128)(2,1)} %all-gather.18.cloned.1.call-done, s32[]{:T(128)S(6)} %select_n.140), kind=kLoop, calls=%fused_computation.88 | loop fusion | bytes 33554436 | tf_op jit(solution)/shard_map/dynamic_slice | solution.py:211
  1026.6 6.5 constant_dynamic-slice_fusion
  1033.1 3.3 constant_dynamic-update-slice_fusion.4
  1036.4 3.2 constant_dynamic-update-slice_fusion.3
  1039.6 222.7 %collective-permute-done.2 = bf16[2,512,2048]{2,1,0:T(8,128)(2,1)} collective-permute-done((bf16[2,512,2048]{2,1,0:T(8,128)(2,1)}, bf16[2,512,2048]{2,1,0:T(8,128)(2,1)}, u32[]{:S(2)}, u32[]{:S(2)}) %collective-permute-start.2) | collective-permute-done | bytes 4194336 | tf_op jit(solution)/shard_map/ppermute | solution.py:255
  1262.3 4.8 constant_dynamic-update-slice_fusion.2
  1267.1 4.8 constant_dynamic-update-slice_fusion.1
  1271.9 2.3 constant_dynamic-update-slice_fusion
  (53 shorter events, 0.2 us)
Async XLA Ops:
  7.2 1.9 copy-start
  7.2 59.9 %all-gather.12.cloned.1.call-start = ((), (), s32[]{:S(2)}) async-start(), calls=%async_computation.2 | async-start | bytes 9437184 | tf_op jit(solution)/shard_map/all_gather | solution.py:212
  13.7 11.1 copy-start.5
  13.7 11.7 copy-start.6
  13.8 106.1 %all-gather.10.cloned.1.call-start = ((), (), s32[]{:S(2)}) async-start(), calls=%async_computation.1 | async-start | bytes 9437184 | tf_op jit(solution)/shard_map/all_gather | solution.py:212
  14.5 214.7 %all-gather.8.cloned.1.call-start = ((), (), s32[]{:S(2)}) async-start(), calls=%async_computation | async-start | bytes 9437184 | tf_op jit(solution)/shard_map/all_gather | solution.py:212
  15.2 360.8 %all-gather.14.cloned.1.call-start = ((), (), s32[]{:S(2)}) async-start(), calls=%async_computation.3 | async-start | bytes 9437184 | tf_op jit(solution)/shard_map/all_gather | solution.py:213
  15.8 460.5 %all-gather.16.cloned.1.call-start = ((), (), s32[]{:S(2)}) async-start(), calls=%async_computation.4 | async-start | bytes 37748736 | tf_op jit(solution)/shard_map/all_gather | solution.py:212
  22.1 609.0 %all-gather.18.cloned.1.call-start = ((), (), s32[]{:S(2)}) async-start(), calls=%async_computation.5 | async-start | bytes 37748736 | tf_op jit(solution)/shard_map/all_gather | solution.py:212
  22.7 769.0 %all-gather.20.cloned.1.call-start = ((), (), s32[]{:S(2)}) async-start(), calls=%async_computation.6 | async-start | bytes 37748736 | tf_op jit(solution)/shard_map/all_gather | solution.py:213
  25.4 13.7 %copy-start.7 = (s32[16]{0:T(128)S(1)}, s32[16]{0:T(128)}, u32[]{:S(2)}) copy-start(s32[16]{0:T(128)} %len_ref.1) | copy-start | bytes 196
  69.7 2.0 copy-start.2
  122.4 2.0 copy-start.3
  124.5 65.3 %slice-start.8 = ((s8[8388608]{0:T(1024)(128)(4,1)}), s8[4194304]{0:T(1024)(128)(4,1)S(1)}, s32[]{:S(2)}) async-start(s8[8388608]{0:T(1024)(128)(4,1)} %bitcast.101), calls=%async_computation.15 | async-start | bytes 8388608
  147.4 42.4 %slice-start.9 = ((s8[8388608]{0:T(1024)(128)(4,1)}), s8[4194304]{0:T(1024)(128)(4,1)S(1)}, s32[]{:S(2)}) async-start(s8[8388608]{0:T(1024)(128)(4,1)} %bitcast.101), calls=%async_computation.16 | async-start | bytes 8388608
  466.5 9.8 copy-start.4
  853.0 183.5 %collective-permute-start.1 = (bf16[1,512,2048]{2,1,0:T(8,128)(2,1)}, bf16[1,512,2048]{2,1,0:T(8,128)(2,1)}, u32[]{:S(2)}, u32[]{:S(2)}) collective-permute-start(bf16[1,512,2048]{2,1,0:T(8,128)(2,1)} %get-tuple-element.29), channel_id=1, source_target_pairs={{0,4},{4,0},{1,5},{5,1},{2,6},{6,2},{3,7},{7,3}} | collective-permute-start | bytes 6291464 | tf_op jit(solution)/shard_map/ppermute | solution.py:255
  853.1 180.1 %collective-permute-start = (bf16[1,512,2048]{2,1,0:T(8,128)(2,1)}, bf16[1,512,2048]{2,1,0:T(8,128)(2,1)}, u32[]{:S(2)}, u32[]{:S(2)}) collective-permute-start(bf16[1,512,2048]{2,1,0:T(8,128)(2,1)} %get-tuple-element.27), channel_id=1, source_target_pairs={{0,4},{4,0},{1,5},{5,1},{2,6},{6,2},{3,7},{7,3}} | collective-permute-start | bytes 6291464 | tf_op jit(solution)/shard_map/ppermute | solution.py:255
  990.5 281.4 %collective-permute-start.4 = (bf16[2,512,2048]{2,1,0:T(8,128)(2,1)}, bf16[2,512,2048]{2,1,0:T(8,128)(2,1)S(1)}, u32[]{:S(2)}, u32[]{:S(2)}) collective-permute-start(bf16[2,512,2048]{2,1,0:T(8,128)(2,1)} %get-tuple-element.35), channel_id=1, source_target_pairs={{0,4},{4,0},{1,5},{5,1},{2,6},{6,2},{3,7},{7,3}} | collective-permute-start | bytes 12582920 | tf_op jit(solution)/shard_map/ppermute | solution.py:255
  990.5 276.6 %collective-permute-start.3 = (bf16[2,512,2048]{2,1,0:T(8,128)(2,1)}, bf16[2,512,2048]{2,1,0:T(8,128)(2,1)}, u32[]{:S(2)}, u32[]{:S(2)}) collective-permute-start(bf16[2,512,2048]{2,1,0:T(8,128)(2,1)} %get-tuple-element.33), channel_id=1, source_target_pairs={{0,4},{4,0},{1,5},{5,1},{2,6},{6,2},{3,7},{7,3}} | collective-permute-start | bytes 12582920 | tf_op jit(solution)/shard_map/ppermute | solution.py:255
  992.5 269.8 %collective-permute-start.2 = (bf16[2,512,2048]{2,1,0:T(8,128)(2,1)}, bf16[2,512,2048]{2,1,0:T(8,128)(2,1)}, u32[]{:S(2)}, u32[]{:S(2)}) collective-permute-start(bf16[2,512,2048]{2,1,0:T(8,128)(2,1)} %get-tuple-element.31), channel_id=1, source_target_pairs={{0,4},{4,0},{1,5},{5,1},{2,6},{6,2},{3,7},{7,3}} | collective-permute-start | bytes 12582920 | tf_op jit(solution)/shard_map/ppermute | solution.py:255
  992.6 34.0 %slice-start = ((s8[33554432]{0:T(1024)(128)(4,1)}), s8[4194304]{0:T(1024)(128)(4,1)S(1)}, s32[]{:S(2)}) async-start(s8[33554432]{0:T(1024)(128)(4,1)} %bitcast.99), calls=%async_computation.7 | async-start | bytes 8388608
  992.6 34.0 %slice-start.1 = ((s8[33554432]{0:T(1024)(128)(4,1)}), s8[4194304]{0:T(1024)(128)(4,1)S(1)}, s32[]{:S(2)}) async-start(s8[33554432]{0:T(1024)(128)(4,1)} %bitcast.99), calls=%async_computation.8 | async-start | bytes 8388608
  992.6 34.0 %slice-start.2 = ((s8[33554432]{0:T(1024)(128)(4,1)}), s8[4194304]{0:T(1024)(128)(4,1)S(1)}, s32[]{:S(2)}) async-start(s8[33554432]{0:T(1024)(128)(4,1)} %bitcast.99), calls=%async_computation.9 | async-start | bytes 8388608
  992.6 34.0 %slice-start.3 = ((s8[33554432]{0:T(1024)(128)(4,1)}), s8[4194304]{0:T(1024)(128)(4,1)S(1)}, s32[]{:S(2)}) async-start(s8[33554432]{0:T(1024)(128)(4,1)} %bitcast.99), calls=%async_computation.10 | async-start | bytes 8388608
  1009.5 17.0 %slice-start.4 = ((s8[33554432]{0:T(1024)(128)(4,1)}), s8[4194304]{0:T(1024)(128)(4,1)S(1)}, s32[]{:S(2)}) async-start(s8[33554432]{0:T(1024)(128)(4,1)} %bitcast.99), calls=%async_computation.11 | async-start | bytes 8388608
  1009.5 17.0 %slice-start.5 = ((s8[33554432]{0:T(1024)(128)(4,1)}), s8[4194304]{0:T(1024)(128)(4,1)S(1)}, s32[]{:S(2)}) async-start(s8[33554432]{0:T(1024)(128)(4,1)} %bitcast.99), calls=%async_computation.12 | async-start | bytes 8388608
  1009.5 17.0 %slice-start.6 = ((s8[33554432]{0:T(1024)(128)(4,1)}), s8[4194304]{0:T(1024)(128)(4,1)S(1)}, s32[]{:S(2)}) async-start(s8[33554432]{0:T(1024)(128)(4,1)} %bitcast.99), calls=%async_computation.13 | async-start | bytes 8388608
  1009.5 17.0 %slice-start.7 = ((s8[33554432]{0:T(1024)(128)(4,1)}), s8[4194304]{0:T(1024)(128)(4,1)S(1)}, s32[]{:S(2)}) async-start(s8[33554432]{0:T(1024)(128)(4,1)} %bitcast.99), calls=%async_computation.14 | async-start | bytes 8388608
  1033.1 241.1 %copy-start.1 = (bf16[2048,768]{1,0:T(8,128)(2,1)S(1)}, bf16[2048,768]{1,0:T(8,128)(2,1)}, u32[]{:S(2)}) copy-start(bf16[2048,768]{1,0:T(8,128)(2,1)} %param.14) | copy-start | bytes 9437188
Sparse Core Ops, SparseCore 0:
  13.9 53.1 all-gather.11
  69.4 50.3 all-gather.9
  122.2 50.3 all-gather.7
  174.2 48.6 all-gather.13
  224.6 155.0 all-gather.15
  381.5 155.0 all-gather.17
  538.4 155.0 all-gather.19

commit v3 on v2

--- a/solution.py
+++ b/solution.py
@@ -19,7 +19,7 @@
 BF16 = jnp.bfloat16
 F32 = jnp.float32
 SHARED = 0
-CHUNKS = (1, 1, 2, 2, 2)
+CHUNKS = (1, 2, 2, 2, 1)
 
 
 def rms_norm(x_in, gain_vec):
@@ -214,15 +214,17 @@
 
         wq, wk, wv = unpack_qkv(w_qkv, head_dim)
         ff = w_gate_up.shape[1] // 2
-        wk = cols(wk)
-        wv = cols(wv)
+        wkv = with_layout_constraint(lax.all_gather(jnp.stack([wk, wv]), axes, axis=2, tiled=True), Layout((0, 1, 2)))
+        wk, wv = wkv[0], wkv[1]
         wq = cols(wq)
         wo = rows(w_o)
         wgate = cols(w_gate_up[:, :ff])
         wup = cols(w_gate_up[:, ff:])
         wdown = rows(w_down)
         share = lambda w, axis: take(w, mine * (w.shape[axis] // n_tpa), w.shape[axis] // n_tpa, axis)
-        out_w = (share(wq, 1), share(wk, 1), share(wv, 1), share(wo, 0), share(wgate, 1), share(wup, 1), share(wdown, 0))
+        n_cols = wkv.shape[2] // n_tpa
+        part_of = lambda k: lax.dynamic_slice(wkv, (k, 0, mine * n_cols), (1, wkv.shape[1], n_cols))[0]
+        out_w = (share(wq, 1), part_of(0), part_of(1), share(wo, 0), share(wgate, 1), share(wup, 1), share(wdown, 0))
 
         angles = rope_angles(seq, head_dim)
         u = rms_norm(x_loc, g_attn)

time: 1290 us -> 1390 us (1.078)
  waiting for transfers between devices: 255 us -> 363 us
    ppermute x5, waiting for transfers between devices: 223 us -> 270 us  [local_step(): other = lax.ppermute(part, 'tpa', swap)]
    all_gather x2, waiting for transfers between devices: 0.01 us -> 45.9 us  [local_step(): rows = lambda w: lax.all_gather(w, axes, axis=0, tiled=True)]
    all_gather x0 -> x1, waiting for transfers between devices: none -> 42.2 us  [local_step(): lax.all_gather(jnp.stack([wk, wv]), axes, axis=2, tiled=True)]
    all_gather x5 -> x3, waiting for transfers between devices: 28.7 us -> 3.58 us  [local_step(): lax.all_gather(w, axes, axis=1, tiled=True)]
    dynamic_slice x8 -> x6, local copies, waits for them, and re-layouts: 56.1 us -> 50.5 us  [local_step(): take = lambda arr, at, n, axis=0: lax.dynamic_slice_in_dim(arr, at, n, axis)]
  transfers between devices with their start and end apart: 12 -> 11, of which waited for: 3 -> 4; matrix products, arithmetic and copies ran while one was open for 61% -> 59% of each run, Pallas kernels for 12% -> 11%
where the time goes in v3:
time: 1390 us
  matrix products  722 us (52%)
  waiting for transfers between devices  363 us (26%)
  Pallas kernels  148 us (11%)
  local copies, waits for them, and re-layouts  98.5 us (7%)
  other arithmetic  39 us (3%)
  between operations  14.6 us (1%)
    dot_general x13, matrix products, matmul(): return jnp.einsum('bsd,dc->bsc', lhs, rhs, preferred_element_type=F32)  719 us
    ppermute x5, waiting for transfers between devices, local_step(): other = lax.ppermute(part, 'tpa', swap)  270 us
    pallas_call x1, Pallas kernels, attention(): pl.pallas_call(functools.partial(attn_kernel, half=half, blk=256), grid_s...  103 us
    dynamic_slice x6, local copies, waits for them, and re-layouts, local_step(): take = lambda arr, at, n, axis=0: lax.dynamic_slice_in_dim(arr, at, n, axis)  50.5 us
    all_gather x2, waiting for transfers between devices, local_step(): rows = lambda w: lax.all_gather(w, axes, axis=0, tiled=True)  45.9 us
    pallas_call x1, Pallas kernels, fill_cache(): pl.pallas_call(functools.partial(cache_kernel, n_own=n_own), grid_spec=pl...  44.4 us
    all_gather x1, waiting for transfers between devices, local_step(): lax.all_gather(jnp.stack([wk, wv]), axes, axis=2, tiled=True)  42.2 us
  transfers between devices with their start and end apart: 11, of which 4 were waited for; matrix products, arithmetic and copies ran while one was open for 59% of the time, Pallas kernels for 11%

profile of v3, /device:TPU:0, one launch (start us, length us, event | category | flops | bytes accessed | tf_op | source)
XLA Modules:
  0.0 1389.4 jit_solution(4396050694590909203)
XLA Ops:
  7.2 0.0 copy-start
  7.2 0.0 all-gather.7.cloned.1.call-start
  7.3 1.8 copy-done
  9.1 2.9 fusion.51
  12.0 1.2 slice_bitcast_fusion.13
  13.2 0.0 all-gather.7.cloned.1.call-update
  13.2 0.0 all-gather.11.cloned.1.call-start
  13.2 0.7 all-gather.11.cloned.1.call-update
  13.9 0.0 all-gather.9.cloned.1.call-start
  14.0 1.5 pad_maximum_fusion
  15.5 0.0 all-gather.9.cloned.1.call-update
  15.5 0.0 all-gather.13.cloned.1.call-start
  15.6 6.3 fusion.82
  21.8 0.0 all-gather.13.cloned.1.call-update
  21.9 0.0 all-gather.15.cloned.1.call-start
  21.9 0.5 all-gather.15.cloned.1.call-update
  22.5 0.6 all-gather.17.cloned.1.call-start
  23.0 0.0 all-gather.17.cloned.1.call-update
  23.1 1.0 fusion.53
  24.1 0.3 fusion.57
  24.4 0.6 convert_element_type.115
  25.0 11.3 fusion.5
  36.4 0.8 copy.28.cos_ref
  37.3 0.8 copy.29.sin_ref
  38.1 0.6 dynamic_slice.64.len_ref
  38.7 23.6 %fusion.7 = bf16[16,512,2048]{2,1,0:T(8,128)(2,1)} fusion(bf16[16,512,2048]{2,1,0:T(8,128)(2,1)} %param.10, f32[2048]{0:T(1024)S(1)} %convert_element_type.103, f32[16,512]{1,0:T(8,128)S(1)} %add_rsqrt_fusion), kind=kLoop, calls=%fused_computation.11 | loop fusion | flops 67108864 | bytes 67149824 | tf_op jit(solution)/shard_map/convert_element_type | solution.py:28
  62.3 0.7 pad_add_fusion.pos_ref
  62.9 3.6 all-gather.7.cloned.1.call-done
  66.5 4.6 constant_dynamic-slice_fusion.4
  71.1 45.9 %all-gather.11.cloned.1.call-done = bf16[2048,2048]{1,0:T(8,128)(2,1)} async-done(((bf16[256,2048]{1,0:T(8,128)(2,1)}), bf16[2048,2048]{1,0:T(8,128)(2,1)}) %all-gather.11.cloned.1.call-update) | async-done | bytes 8388624 | tf_op jit(solution)/shard_map/all_gather | solution.py:213
  117.0 4.8 constant_dynamic-slice_fusion.3
  121.8 42.9 %convolution_convert_fusion.2.q_ref = bf16[8,512,2048]{2,1,0:T(8,128)(2,1)} fusion(bf16[16,512,2048]{2,1,0:T(8,128)(2,1)} %fusion.7, s32[]{:T(128)S(6)} %select_n.123, bf16[2048,2048]{1,0:T(8,128)(2,1)} %all-gather.7.cloned.1.call-done), kind=kOutput, calls=%fused_computation.33 | convolution fusion | flops 34368126976 | bytes 41943044 | tf_op jit(solution)/shard_map/bsd,dc->bsc/dot_general | solution.py:42
  164.8 42.2 %all-gather.9.cloned.1.call-done = bf16[2,2048,2048]{2,1,0:T(8,128)(2,1)} async-done(((bf16[2,2048,256]{2,1,0:T(8,128)(2,1)}), bf16[2,2048,2048]{2,1,0:T(8,128)(2,1)}) %all-gather.9.cloned.1.call-update) | async-done | bytes 16777232 | tf_op jit(solution)/shard_map/all_gather | solution.py:217
  206.9 41.9 %convolution_convert_fusion.1 = bf16[8,512,2048]{1,2,0:T(8,128)(2,1)} fusion(bf16[16,512,2048]{2,1,0:T(8,128)(2,1)} %fusion.7, s32[]{:T(128)S(6)} %select_n.123, bf16[2,2048,2048]{2,1,0:T(8,128)(2,1)} %all-gather.9.cloned.1.call-done), kind=kOutput, calls=%fused_computation.32 | convolution fusion | flops 34368126976 | bytes 41943044 | tf_op jit(solution)/shard_map/bsd,dc->bsc/dot_general | solution.py:42
  248.8 42.0 %convolution_convert_fusion = bf16[8,512,2048]{1,2,0:T(8,128)(2,1)} fusion(bf16[16,512,2048]{2,1,0:T(8,128)(2,1)} %fusion.7, s32[]{:T(128)S(6)} %select_n.123, bf16[2,2048,2048]{2,1,0:T(8,128)(2,1)} %all-gather.9.cloned.1.call-done), kind=kOutput, calls=%fused_computation.31 | convolution fusion | flops 34368126976 | bytes 41943044 | tf_op jit(solution)/shard_map/bsd,dc->bsc/dot_general | solution.py:42
  290.8 103.2 %prefill_attention.1 = bf16[8,512,2048]{2,1,0:T(8,128)(2,1)} custom-call(s32[8]{0:T(128)} %dynamic_slice.64.len_ref, bf16[8,512,2048]{2,1,0:T(8,128)(2,1)} %convolution_convert_fusion.2.q_ref, bf16[8,2048,512]{2,1,0:T(8,128)(2,1)} %bitcast.121, bf16[8,2048,512]{2,1,0:T(8,128)(2,1)} %bitcast.123, f32[512,128]{1,0:T(8,128)} %copy.28.cos_ref, ...), custom_call_target="tpu_custom_call" | custom-call | flops 68719476736 | bytes 67108864 | tf_op jit(solution)/shard_map/prefill_attention/pallas_call | solution.py:107
  394.1 23.2 %fusion.36 = bf16[8,512,1024]{1,2,0:T(8,128)(2,1)} fusion(bf16[16,512,2048]{2,1,0:T(8,128)(2,1)} %fusion.7, s32[]{:T(128)S(6)} %select_n.134, bf16[2,2048,2048]{2,1,0:T(8,128)(2,1)} %all-gather.9.cloned.1.call-done, s32[]{:T(128)S(6)} %select_n.139), kind=kOutput, calls=%fused_computation.49 | convolution fusion | flops 17184063488 | bytes 29360136 | tf_op jit(solution)/shard_map/bsd,dc->bsc/dot_general | solution.py:42
  417.3 23.3 %fusion.33 = bf16[8,512,1024]{1,2,0:T(8,128)(2,1)} fusion(bf16[16,512,2048]{2,1,0:T(8,128)(2,1)} %fusion.7, s32[]{:T(128)S(6)} %select_n.134, bf16[2,2048,2048]{2,1,0:T(8,128)(2,1)} %all-gather.9.cloned.1.call-done, s32[]{:T(128)S(6)} %select_n.139), kind=kOutput, calls=%fused_computation.48 | convolution fusion | flops 17184063488 | bytes 29360136 | tf_op jit(solution)/shard_map/bsd,dc->bsc/dot_general | solution.py:42
  440.6 44.4 %fill_cache.1 = (bf16[16,16,64,512]{3,2,1,0:T(8,128)(2,1)}, bf16[16,16,64,512]{3,2,1,0:T(8,128)(2,1)}) custom-call(s32[3]{0:T(128)} %pad_add_fusion.pos_ref, s32[16]{0:T(128)} %len_ref.1, bf16[8,32,64,512]{3,2,1,0:T(8,128)(2,1)} %bitcast.122, bf16[8,32,64,512]{3,2,1,0:T(8,128)(2,1)} %bitcast.124, bf16[8,16,64,512]{3,2,1,0:T(8,128)(2,1)} %bitcast.126, ...), custom_call_target="tpu_custom_call" | custom-call | flops 40000000000 | bytes 100663296 | tf_op jit(solution)/shard_map/fill_cache/pallas_call | solution.py:174
  485.0 44.9 %fusion.8 = (f32[8,512]{1,0:T(8,128)S(1)}, bf16[8,512,2048]{2,1,0:T(8,128)(2,1)}) fusion(bf16[8,512,2048]{2,1,0:T(8,128)(2,1)} %prefill_attention.1, bf16[2048,2048]{1,0:T(8,128)(2,1)} %all-gather.11.cloned.1.call-done, bf16[16,512,2048]{2,1,0:T(8,128)(2,1)} %param.10, s32[]{:T(128)S(6)} %select_n.123), kind=kOutput, calls=%fused_computation.14 | convolution fusion | flops 34410065920 | bytes 58736644 | tf_op jit(solution)/shard_map/bsd,dc->bsc/dot_general | solution.py:42
  529.9 9.2 dynamic-slice_bitcast_fusion
  539.0 154.7 %fusion.18 = bf16[8,512,8192]{2,1,0:T(8,128)(2,1)} fusion(bf16[2048,8192]{1,0:T(8,128)(2,1)} %all-gather.13.cloned.1.call-done, bf16[8,512,2048]{2,1,0:T(8,128)(2,1)} %get-tuple-element.37, f32[2048]{0:T(1024)S(1)} %copy-done.2, f32[8,512]{1,0:T(8,128)S(1)} %add_rsqrt_fusion.1), kind=kOutput, calls=%fused_computation.24 | convolution fusion | flops 137472507904 | bytes 117465088 | tf_op jit(solution)/shard_map/bsd,dc->bsc/dot_general | solution.py:42
  693.7 160.5 %fusion.4 = bf16[8,512,8192]{2,1,0:T(8,128)(2,1)} fusion(bf16[8,512,8192]{2,1,0:T(8,128)(2,1)} %fusion.18, bf16[2048,8192]{1,0:T(8,128)(2,1)} %all-gather.15.cloned.1.call-done, bf16[8,512,2048]{2,1,0:T(8,128)(2,1)} %get-tuple-element.37, f32[2048]{0:T(1024)S(1)} %copy-done.2, f32[8,512]{1,0:T(8,128)S(1)} %add_rsqrt_fusion.1), kind=kOutput, calls=%fused_computation.6 | convolution fusion | flops 137774497792 | bytes 184573952 | tf_op jit(solution)/shard_map/bsd,dc->bsc/dot_general | solution.py:42
  854.2 11.2 broadcast_in_dim.2
  865.4 24.9 %constant_dynamic-update-slice_fusion.9 = (bf16[16,512,2048]{2,1,0:T(8,128)(2,1)}, bf16[1,512,2048]{2,1,0:T(8,128)(2,1)}) fusion(bf16[16,512,2048]{2,1,0:T(8,128)(2,1)} %broadcast_in_dim.2, s32[]{:T(128)S(6)} %select_n.123, bf16[8192,2048]{1,0:T(8,128)(2,1)} %all-gather.17.cloned.1.call-done, bf16[8,512,8192]{2,1,0:T(8,128)(2,1)} %fusion.4, ...), kind=kOutput, calls=%fused_computation.109 | convolution fusion | flops 17183014912 | bytes 48234500 | tf_op jit(solution)/shard_map/bsd,dc->bsc/dot_general | solution.py:42
  890.3 0.3 collective-permute-start
  890.6 45.3 %constant_dynamic-update-slice_fusion.8 = (bf16[16,512,2048]{2,1,0:T(8,128)(2,1)}, bf16[2,512,2048]{2,1,0:T(8,128)(2,1)}) fusion(bf16[16,512,2048]{2,1,0:T(8,128)(2,1)} %get-tuple-element.38, s32[]{:T(128)S(6)} %select_n.130, bf16[8,512,8192]{2,1,0:T(8,128)(2,1)} %fusion.4, bf16[8192,2048]{1,0:T(8,128)(2,1)} %all-gather.17.cloned.1.call-done, ...), kind=kOutput, calls=%fused_computation.108 | convolution fusion | flops 34366029824 | bytes 113246208 | tf_op jit(solution)/shard_map/bsd,dc->bsc/dot_general | solution.py:42
  935.9 45.1 %constant_dynamic-update-slice_fusion.7 = (bf16[16,512,2048]{2,1,0:T(8,128)(2,1)}, bf16[2,512,2048]{2,1,0:T(8,128)(2,1)}) fusion(bf16[16,512,2048]{2,1,0:T(8,128)(2,1)} %get-tuple-element.40, s32[]{:T(128)S(6)} %select_n.131, bf16[8,512,8192]{2,1,0:T(8,128)(2,1)} %fusion.4, bf16[8192,2048]{1,0:T(8,128)(2,1)} %all-gather.17.cloned.1.call-done, ...), kind=kOutput, calls=%fused_computation.107 | convolution fusion | flops 34366029824 | bytes 113246208 | tf_op jit(solution)/shard_map/bsd,dc->bsc/dot_general | solution.py:42
  981.0 45.3 %constant_dynamic-update-slice_fusion.6 = (bf16[16,512,2048]{2,1,0:T(8,128)(2,1)}, bf16[2,512,2048]{2,1,0:T(8,128)(2,1)}) fusion(bf16[16,512,2048]{2,1,0:T(8,128)(2,1)} %get-tuple-element.42, s32[]{:T(128)S(6)} %select_n.132, bf16[8,512,8192]{2,1,0:T(8,128)(2,1)} %fusion.4, bf16[8192,2048]{1,0:T(8,128)(2,1)} %all-gather.17.cloned.1.call-done, ...), kind=kOutput, calls=%fused_computation.106 | convolution fusion | flops 34366029824 | bytes 113246208 | tf_op jit(solution)/shard_map/bsd,dc->bsc/dot_general | solution.py:42
  1026.3 24.9 %constant_dynamic-update-slice_fusion.5 = (bf16[16,512,2048]{2,1,0:T(8,128)(2,1)}, bf16[1,512,2048]{2,1,0:T(8,128)(2,1)}) fusion(bf16[16,512,2048]{2,1,0:T(8,128)(2,1)} %get-tuple-element.44, s32[]{:T(128)S(6)} %select_n.133, bf16[8192,2048]{1,0:T(8,128)(2,1)} %all-gather.17.cloned.1.call-done, bf16[8,512,8192]{2,1,0:T(8,128)(2,1)} %fusion.4, ...), kind=kOutput, calls=%fused_computation.105 | convolution fusion | flops 17183014912 | bytes 48234500 | tf_op jit(solution)/shard_map/bsd,dc->bsc/dot_general | solution.py:42
  1051.2 1.7 collective-permute-start.4
  1052.9 0.3 collective-permute-start.3
  1053.3 1.7 collective-permute-start.2
  1054.9 0.3 collective-permute-start.1
  1055.3 17.0 %constant_dynamic-slice_fusion.2 = bf16[2048,4096]{1,0:T(8,128)(2,1)} fusion(bf16[2048,8192]{1,0:T(8,128)(2,1)} %all-gather.13.cloned.1.call-done, s32[]{:T(128)S(6)} %select_n.140), kind=kLoop, calls=%fused_computation.96 | loop fusion | bytes 33554436 | tf_op jit(solution)/shard_map/dynamic_slice | solution.py:211
  1072.3 17.0 %constant_dynamic-slice_fusion.1 = bf16[2048,4096]{1,0:T(8,128)(2,1)} fusion(bf16[2048,8192]{1,0:T(8,128)(2,1)} %all-gather.15.cloned.1.call-done, s32[]{:T(128)S(6)} %select_n.140), kind=kLoop, calls=%fused_computation.95 | loop fusion | bytes 33554436 | tf_op jit(solution)/shard_map/dynamic_slice | solution.py:211
  1089.3 6.5 constant_dynamic-slice_fusion
  1095.8 3.3 constant_dynamic-update-slice_fusion.4
  1099.2 269.8 %collective-permute-done.1 = bf16[2,512,2048]{2,1,0:T(8,128)(2,1)} collective-permute-done((bf16[2,512,2048]{2,1,0:T(8,128)(2,1)}, bf16[2,512,2048]{2,1,0:T(8,128)(2,1)}, u32[]{:S(2)}, u32[]{:S(2)}) %collective-permute-start.1) | collective-permute-done | bytes 4194336 | tf_op jit(solution)/shard_map/ppermute | solution.py:257
  1369.0 4.8 constant_dynamic-update-slice_fusion.3
  1373.7 0.0 collective-permute-done.2
  1373.7 4.8 constant_dynamic-update-slice_fusion.2
  1378.5 2.3 constant_dynamic-update-slice_fusion.1
  1380.9 1.5 constant_dynamic-update-slice_fusion
  (41 shorter events, 0.2 us)
Async XLA Ops:
  7.2 1.9 copy-start
  7.2 59.3 %all-gather.7.cloned.1.call-start = ((), (), s32[]{:S(2)}) async-start(), calls=%async_computation | async-start | bytes 9437184 | tf_op jit(solution)/shard_map/all_gather | solution.py:212
  13.2 103.9 %all-gather.11.cloned.1.call-start = ((), (), s32[]{:S(2)}) async-start(), calls=%async_computation.2 | async-start | bytes 9437184 | tf_op jit(solution)/shard_map/all_gather | solution.py:213
  13.9 193.0 %all-gather.9.cloned.1.call-start = ((), (), s32[]{:S(2)}) async-start(), calls=%async_computation.1 | async-start | bytes 18874368 | tf_op jit(solution)/shard_map/all_gather | solution.py:217
  15.5 8.9 copy-start.3
  15.5 9.5 copy-start.4
  15.5 523.5 %all-gather.13.cloned.1.call-start = ((), (), s32[]{:S(2)}) async-start(), calls=%async_computation.3 | async-start | bytes 37748736 | tf_op jit(solution)/shard_map/all_gather | solution.py:212
  21.9 671.8 %all-gather.15.cloned.1.call-start = ((), (), s32[]{:S(2)}) async-start(), calls=%async_computation.4 | async-start | bytes 37748736 | tf_op jit(solution)/shard_map/all_gather | solution.py:212
  22.5 831.8 %all-gather.17.cloned.1.call-start = ((), (), s32[]{:S(2)}) async-start(), calls=%async_computation.5 | async-start | bytes 37748736 | tf_op jit(solution)/shard_map/all_gather | solution.py:213
  25.0 13.1 copy-start.5
  529.8 9.2 copy-start.2
  890.3 205.5 %collective-permute-start = (bf16[1,512,2048]{2,1,0:T(8,128)(2,1)}, bf16[1,512,2048]{2,1,0:T(8,128)(2,1)}, u32[]{:S(2)}, u32[]{:S(2)}) collective-permute-start(bf16[1,512,2048]{2,1,0:T(8,128)(2,1)} %get-tuple-element.39), channel_id=1, source_target_pairs={{0,4},{4,0},{1,5},{5,1},{2,6},{6,2},{3,7},{7,3}} | collective-permute-start | bytes 6291464 | tf_op jit(solution)/shard_map/ppermute | solution.py:257
  1051.2 329.6 %collective-permute-start.4 = (bf16[1,512,2048]{2,1,0:T(8,128)(2,1)}, bf16[1,512,2048]{2,1,0:T(8,128)(2,1)S(1)}, u32[]{:S(2)}, u32[]{:S(2)}) collective-permute-start(bf16[1,512,2048]{2,1,0:T(8,128)(2,1)} %get-tuple-element.47), channel_id=1, source_target_pairs={{0,4},{4,0},{1,5},{5,1},{2,6},{6,2},{3,7},{7,3}} | collective-permute-start | bytes 6291464 | tf_op jit(solution)/shard_map/ppermute | solution.py:257
  1052.9 325.6 %collective-permute-start.3 = (bf16[2,512,2048]{2,1,0:T(8,128)(2,1)}, bf16[2,512,2048]{2,1,0:T(8,128)(2,1)S(1)}, u32[]{:S(2)}, u32[]{:S(2)}) collective-permute-start(bf16[2,512,2048]{2,1,0:T(8,128)(2,1)} %get-tuple-element.45), channel_id=1, source_target_pairs={{0,4},{4,0},{1,5},{5,1},{2,6},{6,2},{3,7},{7,3}} | collective-permute-start | bytes 12582920 | tf_op jit(solution)/shard_map/ppermute | solution.py:257
  1053.3 320.5 %collective-permute-start.2 = (bf16[2,512,2048]{2,1,0:T(8,128)(2,1)}, bf16[2,512,2048]{2,1,0:T(8,128)(2,1)}, u32[]{:S(2)}, u32[]{:S(2)}) collective-permute-start(bf16[2,512,2048]{2,1,0:T(8,128)(2,1)} %get-tuple-element.43), channel_id=1, source_target_pairs={{0,4},{4,0},{1,5},{5,1},{2,6},{6,2},{3,7},{7,3}} | collective-permute-start | bytes 12582920 | tf_op jit(solution)/shard_map/ppermute | solution.py:257
  1054.9 314.0 %collective-permute-start.1 = (bf16[2,512,2048]{2,1,0:T(8,128)(2,1)}, bf16[2,512,2048]{2,1,0:T(8,128)(2,1)}, u32[]{:S(2)}, u32[]{:S(2)}) collective-permute-start(bf16[2,512,2048]{2,1,0:T(8,128)(2,1)} %get-tuple-element.41), channel_id=1, source_target_pairs={{0,4},{4,0},{1,5},{5,1},{2,6},{6,2},{3,7},{7,3}} | collective-permute-start | bytes 12582920 | tf_op jit(solution)/shard_map/ppermute | solution.py:257
  1055.3 34.0 %slice-start = ((s8[33554432]{0:T(1024)(128)(4,1)}), s8[4194304]{0:T(1024)(128)(4,1)S(1)}, s32[]{:S(2)}) async-start(s8[33554432]{0:T(1024)(128)(4,1)} %bitcast.113), calls=%async_computation.6 | async-start | bytes 8388608
  1055.3 34.0 %slice-start.1 = ((s8[33554432]{0:T(1024)(128)(4,1)}), s8[4194304]{0:T(1024)(128)(4,1)S(1)}, s32[]{:S(2)}) async-start(s8[33554432]{0:T(1024)(128)(4,1)} %bitcast.113), calls=%async_computation.7 | async-start | bytes 8388608
  1055.3 34.0 %slice-start.2 = ((s8[33554432]{0:T(1024)(128)(4,1)}), s8[4194304]{0:T(1024)(128)(4,1)S(1)}, s32[]{:S(2)}) async-start(s8[33554432]{0:T(1024)(128)(4,1)} %bitcast.113), calls=%async_computation.8 | async-start | bytes 8388608
  1055.3 34.0 %slice-start.3 = ((s8[33554432]{0:T(1024)(128)(4,1)}), s8[4194304]{0:T(1024)(128)(4,1)S(1)}, s32[]{:S(2)}) async-start(s8[33554432]{0:T(1024)(128)(4,1)} %bitcast.113), calls=%async_computation.9 | async-start | bytes 8388608
  1072.3 17.0 %slice-start.4 = ((s8[33554432]{0:T(1024)(128)(4,1)}), s8[4194304]{0:T(1024)(128)(4,1)S(1)}, s32[]{:S(2)}) async-start(s8[33554432]{0:T(1024)(128)(4,1)} %bitcast.113), calls=%async_computation.10 | async-start | bytes 8388608
  1072.3 17.0 %slice-start.5 = ((s8[33554432]{0:T(1024)(128)(4,1)}), s8[4194304]{0:T(1024)(128)(4,1)S(1)}, s32[]{:S(2)}) async-start(s8[33554432]{0:T(1024)(128)(4,1)} %bitcast.113), calls=%async_computation.11 | async-start | bytes 8388608
  1072.3 17.0 %slice-start.6 = ((s8[33554432]{0:T(1024)(128)(4,1)}), s8[4194304]{0:T(1024)(128)(4,1)S(1)}, s32[]{:S(2)}) async-start(s8[33554432]{0:T(1024)(128)(4,1)} %bitcast.113), calls=%async_computation.12 | async-start | bytes 8388608
  1072.3 17.0 %slice-start.7 = ((s8[33554432]{0:T(1024)(128)(4,1)}), s8[4194304]{0:T(1024)(128)(4,1)S(1)}, s32[]{:S(2)}) async-start(s8[33554432]{0:T(1024)(128)(4,1)} %bitcast.113), calls=%async_computation.13 | async-start | bytes 8388608
  1095.8 286.5 %copy-start.1 = (bf16[2048,768]{1,0:T(8,128)(2,1)S(1)}, bf16[2048,768]{1,0:T(8,128)(2,1)}, u32[]{:S(2)}) copy-start(bf16[2048,768]{1,0:T(8,128)(2,1)} %param.14) | copy-start | bytes 9437188
Sparse Core Ops, SparseCore 0:
  13.3 53.1 all-gather.6
  68.3 48.6 all-gather.10
  119.4 87.4 all-gather.8
  208.6 155.0 all-gather.12
  365.4 155.0 all-gather.14
  522.3 155.0 all-gather.16

commit v4 on v3

--- a/solution.py
+++ b/solution.py
@@ -18,7 +18,6 @@
 MASK_VALUE = -1e30
 BF16 = jnp.bfloat16
 F32 = jnp.float32
-SHARED = 0
 CHUNKS = (1, 2, 2, 2, 1)
 
 
@@ -203,8 +202,7 @@
     def local_step(x_loc, len_loc, k_buf, v_buf, w_qkv, w_o, w_gate_up, w_down, g_attn, g_mlp):
         batch, seq, _ = x_loc.shape
         _, head_dim = k_buf.shape[2:]
-        n_oth = batch // n_tpa - SHARED // 2
-        n_own = batch - n_oth
+        n_own = n_oth = batch // n_tpa
         mine = lax.axis_index('tpa')
         own_at, oth_at = mine * n_oth, (1 - mine) * n_own
         axes = ('tpa', 'tpb')
@@ -238,8 +236,10 @@
         hidden = (x_own.astype(F32) + matmul(attn, wo)).astype(BF16)
         u2 = rms_norm(hidden, g_mlp)
         gate = matmul(u2, wgate).astype(BF16)
-        up = matmul(u2, wup).astype(BF16)
-        mid = (jax.nn.silu(gate.astype(F32)) * up.astype(F32)).astype(BF16)
+        glu = lambda lo, hi: (jax.nn.silu(gate[lo:hi].astype(F32)) * matmul(u2[lo:hi], wup).astype(BF16).astype(F32)).astype(BF16)
+        late_at = n_own - CHUNKS[-1]
+        mid_first = glu(0, late_at)
+        mid_late = glu(late_at, n_own)
 
         heads_of = lambda t: t.reshape(t.shape[0], t.shape[1] // head_dim, head_dim, seq)
         turn = lambda t: jnp.transpose(t, (0, 2, 3, 1))
@@ -248,20 +248,19 @@
         back = lambda t: jnp.transpose(t, (0, 3, 1, 2))
 
         swap = [(i, n_tpa - 1 - i) for i in range(n_tpa)]
-        sent_at = mine * (n_own - n_oth)
         parts = []
         at = 0
         for n in CHUNKS:
-            local = sent_at + at
-            part = (take(hidden, local, n).astype(F32) + matmul(take(mid, local, n), wdown)).astype(BF16)
+            mid = mid_late if at == late_at else mid_first[at:at + n]
+            part = (hidden[at:at + n].astype(F32) + matmul(mid, wdown)).astype(BF16)
             other = lax.ppermute(part, 'tpa', swap)
-            parts.append((at, local, part, other))
+            parts.append((at, part, other))
             at += n
         assert at == n_oth
         y_out = jnp.zeros(x_loc.shape, BF16)
-        for at, local, part, _ in parts:
-            y_out = lax.dynamic_update_slice_in_dim(y_out, part, own_at + local, 0)
-        for at, local, _, other in parts:
+        for at, part, _ in parts:
+            y_out = lax.dynamic_update_slice_in_dim(y_out, part, own_at + at, 0)
+        for at, _, other in parts:
             y_out = lax.dynamic_update_slice_in_dim(y_out, other, oth_at + at, 0)
         return (y_out, back(k_cache), back(v_cache)) + out_w
 

time: 1390 us -> 1430 us (1.029)
  matrix products: 722 us -> 740 us
  other arithmetic: 39 us -> 54.2 us
    dot_general x13 -> x14, matrix products: 719 us -> 737 us  [matmul(): return jnp.einsum('bsd,dc->bsc', lhs, rhs, preferred_element_type=F32)]
    convert_element_type x1 -> x2, other arithmetic: 23.6 us -> 38.8 us  [rms_norm(): (x_wide * lax.rsqrt(mean_sq + NORM_EPS) * gain_vec.astype(F32)).astype(BF16)]
  transfers between devices with their start and end apart: 11 -> 11, of which waited for: 4 -> 4; matrix products, arithmetic and copies ran while one was open for 59% -> 60% of each run, Pallas kernels for 11% -> 10%
where the time goes in v4:
time: 1430 us; the launch traced here: 1420 us
  matrix products  740 us (52%)
  waiting for transfers between devices  361 us (25%)
  Pallas kernels  148 us (10%)
  local copies, waits for them, and re-layouts  97.1 us (7%)
  other arithmetic  54.2 us (4%)
  between operations  14.5 us (1%)
    dot_general x14, matrix products, matmul(): return jnp.einsum('bsd,dc->bsc', lhs, rhs, preferred_element_type=F32)  737 us
    ppermute x5, waiting for transfers between devices, local_step(): other = lax.ppermute(part, 'tpa', swap)  268 us
    pallas_call x1, Pallas kernels, attention(): pl.pallas_call(functools.partial(attn_kernel, half=half, blk=256), grid_s...  103 us
    dynamic_slice x6, local copies, waits for them, and re-layouts, local_step(): take = lambda arr, at, n, axis=0: lax.dynamic_slice_in_dim(arr, at, n, axis)  50.6 us
    all_gather x2, waiting for transfers between devices, local_step(): rows = lambda w: lax.all_gather(w, axes, axis=0, tiled=True)  45.9 us
    pallas_call x1, Pallas kernels, fill_cache(): pl.pallas_call(functools.partial(cache_kernel, n_own=n_own), grid_spec=pl...  45.1 us
    all_gather x1, waiting for transfers between devices, local_step(): lax.all_gather(jnp.stack([wk, wv]), axes, axis=2, tiled=True)  42.2 us
    convert_element_type x2, other arithmetic, rms_norm(): (x_wide * lax.rsqrt(mean_sq + NORM_EPS) * gain_vec.astype(F32)).astype(BF16)  38.8 us
  transfers between devices with their start and end apart: 11, of which 4 were waited for; matrix products, arithmetic and copies ran while one was open for 60% of the time, Pallas kernels for 10%

profile of v4, /device:TPU:0, one launch (start us, length us, event | category | flops | bytes accessed | tf_op | source)
XLA Modules:
  0.0 1421.9 jit_solution(5122238081451470015)
XLA Ops:
  7.2 0.0 all-gather.7.cloned.1.call-start
  7.3 1.8 copy-done
  9.1 2.9 fusion.58
  12.0 1.2 slice_bitcast_fusion.11
  13.2 0.0 all-gather.7.cloned.1.call-update
  13.2 0.0 all-gather.11.cloned.1.call-start
  13.2 0.7 all-gather.11.cloned.1.call-update
  13.9 0.0 all-gather.9.cloned.1.call-start
  14.0 1.5 pad_maximum_fusion
  15.5 0.0 all-gather.9.cloned.1.call-update
  15.5 0.0 all-gather.13.cloned.1.call-start
  15.6 6.1 fusion.90
  21.7 0.0 all-gather.13.cloned.1.call-update
  21.7 0.0 all-gather.15.cloned.1.call-start
  21.8 0.5 all-gather.15.cloned.1.call-update
  22.3 0.2 all-gather.17.cloned.1.call-start
  22.5 0.3 all-gather.17.cloned.1.call-update
  22.9 1.0 fusion.60
  23.9 0.3 fusion.64
  24.2 0.6 convert_element_type.131
  24.8 11.3 fusion.5
  36.3 0.8 copy.28.cos_ref
  37.1 0.8 copy.29.sin_ref
  38.0 0.7 dynamic_slice.34.len_ref
  38.6 23.6 %fusion.7 = bf16[16,512,2048]{2,1,0:T(8,128)(2,1)} fusion(bf16[16,512,2048]{2,1,0:T(8,128)(2,1)} %param.10, f32[2048]{0:T(1024)S(1)} %convert_element_type.119, f32[16,512]{1,0:T(8,128)S(1)} %add_rsqrt_fusion), kind=kLoop, calls=%fused_computation.11 | loop fusion | flops 67108864 | bytes 67149824 | tf_op jit(solution)/shard_map/convert_element_type | solution.py:27
  62.2 0.6 pad_add_fusion.pos_ref
  62.8 3.6 all-gather.7.cloned.1.call-done
  66.5 4.6 constant_dynamic-slice_fusion.4
  71.1 45.9 %all-gather.11.cloned.1.call-done = bf16[2048,2048]{1,0:T(8,128)(2,1)} async-done(((bf16[256,2048]{1,0:T(8,128)(2,1)}), bf16[2048,2048]{1,0:T(8,128)(2,1)}) %all-gather.11.cloned.1.call-update) | async-done | bytes 8388624 | tf_op jit(solution)/shard_map/all_gather | solution.py:211
  117.0 4.8 constant_dynamic-slice_fusion.3
  121.8 42.9 %convolution_convert_fusion.3.q_ref = bf16[8,512,2048]{2,1,0:T(8,128)(2,1)} fusion(bf16[16,512,2048]{2,1,0:T(8,128)(2,1)} %fusion.7, s32[]{:T(128)S(6)} %select_n.123, bf16[2048,2048]{1,0:T(8,128)(2,1)} %all-gather.7.cloned.1.call-done), kind=kOutput, calls=%fused_computation.40 | convolution fusion | flops 34368126976 | bytes 41943044 | tf_op jit(solution)/shard_map/bsd,dc->bsc/dot_general | solution.py:41
  164.7 42.2 %all-gather.9.cloned.1.call-done = bf16[2,2048,2048]{2,1,0:T(8,128)(2,1)} async-done(((bf16[2,2048,256]{2,1,0:T(8,128)(2,1)}), bf16[2,2048,2048]{2,1,0:T(8,128)(2,1)}) %all-gather.9.cloned.1.call-update) | async-done | bytes 16777232 | tf_op jit(solution)/shard_map/all_gather | solution.py:215
  206.9 41.8 %convolution_convert_fusion.2 = bf16[8,512,2048]{1,2,0:T(8,128)(2,1)} fusion(bf16[16,512,2048]{2,1,0:T(8,128)(2,1)} %fusion.7, s32[]{:T(128)S(6)} %select_n.123, bf16[2,2048,2048]{2,1,0:T(8,128)(2,1)} %all-gather.9.cloned.1.call-done), kind=kOutput, calls=%fused_computation.39 | convolution fusion | flops 34368126976 | bytes 41943044 | tf_op jit(solution)/shard_map/bsd,dc->bsc/dot_general | solution.py:41
  248.8 42.1 %convolution_convert_fusion.1 = bf16[8,512,2048]{1,2,0:T(8,128)(2,1)} fusion(bf16[16,512,2048]{2,1,0:T(8,128)(2,1)} %fusion.7, s32[]{:T(128)S(6)} %select_n.123, bf16[2,2048,2048]{2,1,0:T(8,128)(2,1)} %all-gather.9.cloned.1.call-done), kind=kOutput, calls=%fused_computation.38 | convolution fusion | flops 34368126976 | bytes 41943044 | tf_op jit(solution)/shard_map/bsd,dc->bsc/dot_general | solution.py:41
  290.8 103.2 %prefill_attention.1 = bf16[8,512,2048]{2,1,0:T(8,128)(2,1)} custom-call(s32[8]{0:T(128)} %dynamic_slice.34.len_ref, bf16[8,512,2048]{2,1,0:T(8,128)(2,1)} %convolution_convert_fusion.3.q_ref, bf16[8,2048,512]{2,1,0:T(8,128)(2,1)} %bitcast.154, bf16[8,2048,512]{2,1,0:T(8,128)(2,1)} %bitcast.156, f32[512,128]{1,0:T(8,128)} %copy.28.cos_ref, ...), custom_call_target="tpu_custom_call" | custom-call | flops 68719476736 | bytes 67108864 | tf_op jit(solution)/shard_map/prefill_attention/pallas_call | solution.py:106
  394.0 44.2 %fusion.8 = (f32[8,512]{1,0:T(8,128)S(1)}, bf16[8,512,2048]{2,1,0:T(8,128)(2,1)}) fusion(bf16[8,512,2048]{2,1,0:T(8,128)(2,1)} %prefill_attention.1, bf16[2048,2048]{1,0:T(8,128)(2,1)} %all-gather.11.cloned.1.call-done, bf16[16,512,2048]{2,1,0:T(8,128)(2,1)} %param.10, s32[]{:T(128)S(6)} %select_n.123), kind=kOutput, calls=%fused_computation.15 | convolution fusion | flops 34410065920 | bytes 58736644 | tf_op jit(solution)/shard_map/bsd,dc->bsc/dot_general | solution.py:41
  438.2 23.4 %fusion.41 = bf16[8,512,1024]{1,2,0:T(8,128)(2,1)} fusion(bf16[16,512,2048]{2,1,0:T(8,128)(2,1)} %fusion.7, s32[]{:T(128)S(6)} %select_n.134, bf16[2,2048,2048]{2,1,0:T(8,128)(2,1)} %all-gather.9.cloned.1.call-done, s32[]{:T(128)S(6)} %select_n.139), kind=kOutput, calls=%fused_computation.58 | convolution fusion | flops 17184063488 | bytes 29360136 | tf_op jit(solution)/shard_map/bsd,dc->bsc/dot_general | solution.py:41
  461.6 23.7 %fusion.38 = bf16[8,512,1024]{1,2,0:T(8,128)(2,1)} fusion(bf16[16,512,2048]{2,1,0:T(8,128)(2,1)} %fusion.7, s32[]{:T(128)S(6)} %select_n.134, bf16[2,2048,2048]{2,1,0:T(8,128)(2,1)} %all-gather.9.cloned.1.call-done, s32[]{:T(128)S(6)} %select_n.139), kind=kOutput, calls=%fused_computation.57 | convolution fusion | flops 17184063488 | bytes 29360136 | tf_op jit(solution)/shard_map/bsd,dc->bsc/dot_general | solution.py:41
  485.3 15.2 %fusion.10 = bf16[8,512,2048]{2,1,0:T(8,128)(2,1)} fusion(bf16[8,512,2048]{2,1,0:T(8,128)(2,1)} %get-tuple-element.37, f32[2048]{0:T(1024)S(1)} %copy-done.2, f32[8,512]{1,0:T(8,128)S(1)} %add_rsqrt_fusion.1), kind=kLoop, calls=%fused_computation.17 | loop fusion | flops 33554432 | bytes 33579008 | tf_op jit(solution)/shard_map/convert_element_type | solution.py:27
  500.5 7.8 dynamic-slice_bitcast_fusion
  508.4 45.1 %fill_cache.1 = (bf16[16,16,64,512]{3,2,1,0:T(8,128)(2,1)}, bf16[16,16,64,512]{3,2,1,0:T(8,128)(2,1)}) custom-call(s32[3]{0:T(128)} %pad_add_fusion.pos_ref, s32[16]{0:T(128)} %len_ref.1, bf16[8,32,64,512]{3,2,1,0:T(8,128)(2,1)} %bitcast.155, bf16[8,32,64,512]{3,2,1,0:T(8,128)(2,1)} %bitcast.157, bf16[8,16,64,512]{3,2,1,0:T(8,128)(2,1)} %bitcast.159, ...), custom_call_target="tpu_custom_call" | custom-call | flops 40000000000 | bytes 100663296 | tf_op jit(solution)/shard_map/fill_cache/pallas_call | solution.py:173
  553.5 151.2 %convolution_convert_fusion = bf16[8,512,8192]{2,1,0:T(8,128)(2,1)} fusion(bf16[8,512,2048]{2,1,0:T(8,128)(2,1)} %fusion.10, bf16[2048,8192]{1,0:T(8,128)(2,1)} %all-gather.13.cloned.1.call-done), kind=kOutput, calls=%fused_computation.12 | convolution fusion | flops 137472507904 | bytes 117440512 | tf_op jit(solution)/shard_map/bsd,dc->bsc/dot_general | solution.py:41
  704.7 155.8 %fusion.4 = bf16[7,512,8192]{2,1,0:T(8,128)(2,1)} fusion(bf16[8,512,8192]{2,1,0:T(8,128)(2,1)} %convolution_convert_fusion, bf16[8,512,2048]{2,1,0:T(8,128)(2,1)} %fusion.10, bf16[2048,8192]{1,0:T(8,128)(2,1)} %all-gather.15.cloned.1.call-done), kind=kOutput, calls=%fused_computation.6 | convolution fusion | flops 120523325440 | bytes 167772160 | tf_op jit(solution)/shard_map/bsd,dc->bsc/dot_general | solution.py:41
  860.5 11.2 broadcast_in_dim.2
  871.6 24.9 %constant_dynamic-update-slice_fusion.9 = (bf16[16,512,2048]{2,1,0:T(8,128)(2,1)}, bf16[1,512,2048]{2,1,0:T(8,128)(2,1)}) fusion(bf16[16,512,2048]{2,1,0:T(8,128)(2,1)} %broadcast_in_dim.2, s32[]{:T(128)S(6)} %select_n.123, bf16[8192,2048]{1,0:T(8,128)(2,1)} %all-gather.17.cloned.1.call-done, bf16[7,512,8192]{2,1,0:T(8,128)(2,1)} %fusion.4, ...), kind=kOutput, calls=%fused_computation.119 | convolution fusion | flops 17183014912 | bytes 48234500 | tf_op jit(solution)/shard_map/bsd,dc->bsc/dot_general | solution.py:41
  896.6 2.1 collective-permute-start
  898.6 26.6 %fusion.57.clone.4 = bf16[512,8192]{1,0:T(8,128)(2,1)} fusion(bf16[8,512,8192]{2,1,0:T(8,128)(2,1)} %convolution_convert_fusion, bf16[2048,8192]{1,0:T(8,128)(2,1)} %all-gather.15.cloned.1.call-done, bf16[8,512,2048]{2,1,0:T(8,128)(2,1)} %fusion.10), kind=kOutput, calls=%fused_computation.51.clone.clone.clone.clone.clone.1 | convolution fusion | flops 17217617920 | bytes 52428800 | tf_op jit(solution)/shard_map/bsd,dc->bsc/dot_general | solution.py:41
  925.2 45.1 %constant_dynamic-update-slice_fusion.8 = (bf16[16,512,2048]{2,1,0:T(8,128)(2,1)}, bf16[2,512,2048]{2,1,0:T(8,128)(2,1)}) fusion(bf16[16,512,2048]{2,1,0:T(8,128)(2,1)} %get-tuple-element.38, s32[]{:T(128)S(6)} %select_n.130, bf16[7,512,8192]{2,1,0:T(8,128)(2,1)} %fusion.4, bf16[8192,2048]{1,0:T(8,128)(2,1)} %all-gather.17.cloned.1.call-done, ...), kind=kOutput, calls=%fused_computation.118 | convolution fusion | flops 34366029824 | bytes 104857600 | tf_op jit(solution)/shard_map/bsd,dc->bsc/dot_general | solution.py:41
  970.3 45.2 %constant_dynamic-update-slice_fusion.7 = (bf16[16,512,2048]{2,1,0:T(8,128)(2,1)}, bf16[2,512,2048]{2,1,0:T(8,128)(2,1)}) fusion(bf16[16,512,2048]{2,1,0:T(8,128)(2,1)} %get-tuple-element.40, s32[]{:T(128)S(6)} %select_n.131, bf16[7,512,8192]{2,1,0:T(8,128)(2,1)} %fusion.4, bf16[8192,2048]{1,0:T(8,128)(2,1)} %all-gather.17.cloned.1.call-done, ...), kind=kOutput, calls=%fused_computation.117 | convolution fusion | flops 34366029824 | bytes 104857600 | tf_op jit(solution)/shard_map/bsd,dc->bsc/dot_general | solution.py:41
  1015.6 45.1 %constant_dynamic-update-slice_fusion.6 = (bf16[16,512,2048]{2,1,0:T(8,128)(2,1)}, bf16[2,512,2048]{2,1,0:T(8,128)(2,1)}) fusion(bf16[16,512,2048]{2,1,0:T(8,128)(2,1)} %get-tuple-element.42, s32[]{:T(128)S(6)} %select_n.132, bf16[7,512,8192]{2,1,0:T(8,128)(2,1)} %fusion.4, bf16[8192,2048]{1,0:T(8,128)(2,1)} %all-gather.17.cloned.1.call-done, ...), kind=kOutput, calls=%fused_computation.116 | convolution fusion | flops 34366029824 | bytes 104857600 | tf_op jit(solution)/shard_map/bsd,dc->bsc/dot_general | solution.py:41
  1060.6 25.2 %constant_dynamic-update-slice_fusion.5 = (bf16[16,512,2048]{2,1,0:T(8,128)(2,1)}, bf16[1,512,2048]{2,1,0:T(8,128)(2,1)}) fusion(bf16[16,512,2048]{2,1,0:T(8,128)(2,1)} %get-tuple-element.44, s32[]{:T(128)S(6)} %select_n.133, bf16[8192,2048]{1,0:T(8,128)(2,1)} %all-gather.17.cloned.1.call-done, bf16[8,512,2048]{2,1,0:T(8,128)(2,1)} %get-tuple-element.37, ...), kind=kOutput, calls=%fused_computation.115 | convolution fusion | flops 17183014912 | bytes 48234500 | tf_op jit(solution)/shard_map/bsd,dc->bsc/dot_general | solution.py:41
  1085.8 0.0 collective-permute-start.4
  1085.8 2.0 collective-permute-start.3
  1087.8 0.0 collective-permute-start.2
  1087.9 2.0 collective-permute-start.1
  1089.9 17.0 %constant_dynamic-slice_fusion.2 = bf16[2048,4096]{1,0:T(8,128)(2,1)} fusion(bf16[2048,8192]{1,0:T(8,128)(2,1)} %all-gather.13.cloned.1.call-done, s32[]{:T(128)S(6)} %select_n.140), kind=kLoop, calls=%fused_computation.106 | loop fusion | bytes 33554436 | tf_op jit(solution)/shard_map/dynamic_slice | solution.py:209
  1106.8 17.0 %constant_dynamic-slice_fusion.1 = bf16[2048,4096]{1,0:T(8,128)(2,1)} fusion(bf16[2048,8192]{1,0:T(8,128)(2,1)} %all-gather.15.cloned.1.call-done, s32[]{:T(128)S(6)} %select_n.140), kind=kLoop, calls=%fused_computation.105 | loop fusion | bytes 33554436 | tf_op jit(solution)/shard_map/dynamic_slice | solution.py:209
  1123.9 6.5 constant_dynamic-slice_fusion
  1130.4 3.3 constant_dynamic-update-slice_fusion.4
  1133.7 267.7 %collective-permute-done.1 = bf16[2,512,2048]{2,1,0:T(8,128)(2,1)} collective-permute-done((bf16[2,512,2048]{2,1,0:T(8,128)(2,1)}, bf16[2,512,2048]{2,1,0:T(8,128)(2,1)}, u32[]{:S(2)}, u32[]{:S(2)}) %collective-permute-start.1) | collective-permute-done | bytes 4194336 | tf_op jit(solution)/shard_map/ppermute | solution.py:256
  1401.4 4.8 constant_dynamic-update-slice_fusion.3
  1406.2 4.8 constant_dynamic-update-slice_fusion.2
  1411.0 2.3 constant_dynamic-update-slice_fusion.1
  1413.4 1.5 constant_dynamic-update-slice_fusion
  (43 shorter events, 0.2 us)
Async XLA Ops:
  7.2 1.9 copy-start
  7.2 59.3 %all-gather.7.cloned.1.call-start = ((), (), s32[]{:S(2)}) async-start(), calls=%async_computation | async-start | bytes 9437184 | tf_op jit(solution)/shard_map/all_gather | solution.py:210
  13.2 103.8 %all-gather.11.cloned.1.call-start = ((), (), s32[]{:S(2)}) async-start(), calls=%async_computation.2 | async-start | bytes 9437184 | tf_op jit(solution)/shard_map/all_gather | solution.py:211
  13.9 193.0 %all-gather.9.cloned.1.call-start = ((), (), s32[]{:S(2)}) async-start(), calls=%async_computation.1 | async-start | bytes 18874368 | tf_op jit(solution)/shard_map/all_gather | solution.py:215
  15.5 8.7 copy-start.3
  15.5 8.7 copy-start.4
  15.5 537.9 %all-gather.13.cloned.1.call-start = ((), (), s32[]{:S(2)}) async-start(), calls=%async_computation.3 | async-start | bytes 37748736 | tf_op jit(solution)/shard_map/all_gather | solution.py:210
  21.7 683.0 %all-gather.15.cloned.1.call-start = ((), (), s32[]{:S(2)}) async-start(), calls=%async_computation.4 | async-start | bytes 37748736 | tf_op jit(solution)/shard_map/all_gather | solution.py:210
  22.3 838.2 %all-gather.17.cloned.1.call-start = ((), (), s32[]{:S(2)}) async-start(), calls=%async_computation.5 | async-start | bytes 37748736 | tf_op jit(solution)/shard_map/all_gather | solution.py:211
  24.8 13.1 copy-start.5
  461.6 23.7 %copy-start.2 = (f32[2048]{0:T(1024)S(1)}, f32[2048]{0:T(1024)}, u32[]{:S(2)}) copy-start(f32[2048]{0:T(1024)} %convert_element_type.131) | copy-start | bytes 24580
  896.6 233.8 %collective-permute-start = (bf16[1,512,2048]{2,1,0:T(8,128)(2,1)}, bf16[1,512,2048]{2,1,0:T(8,128)(2,1)}, u32[]{:S(2)}, u32[]{:S(2)}) collective-permute-start(bf16[1,512,2048]{2,1,0:T(8,128)(2,1)} %get-tuple-element.39), channel_id=1, source_target_pairs={{0,4},{4,0},{1,5},{5,1},{2,6},{6,2},{3,7},{7,3}} | collective-permute-start | bytes 6291464 | tf_op jit(solution)/shard_map/ppermute | solution.py:256
  1085.8 327.6 %collective-permute-start.4 = (bf16[1,512,2048]{2,1,0:T(8,128)(2,1)}, bf16[1,512,2048]{2,1,0:T(8,128)(2,1)S(1)}, u32[]{:S(2)}, u32[]{:S(2)}) collective-permute-start(bf16[1,512,2048]{2,1,0:T(8,128)(2,1)} %get-tuple-element.47), channel_id=1, source_target_pairs={{0,4},{4,0},{1,5},{5,1},{2,6},{6,2},{3,7},{7,3}} | collective-permute-start | bytes 6291464 | tf_op jit(solution)/shard_map/ppermute | solution.py:256
  1085.8 325.2 %collective-permute-start.3 = (bf16[2,512,2048]{2,1,0:T(8,128)(2,1)}, bf16[2,512,2048]{2,1,0:T(8,128)(2,1)S(1)}, u32[]{:S(2)}, u32[]{:S(2)}) collective-permute-start(bf16[2,512,2048]{2,1,0:T(8,128)(2,1)} %get-tuple-element.45), channel_id=1, source_target_pairs={{0,4},{4,0},{1,5},{5,1},{2,6},{6,2},{3,7},{7,3}} | collective-permute-start | bytes 12582920 | tf_op jit(solution)/shard_map/ppermute | solution.py:256
  1087.8 318.4 %collective-permute-start.2 = (bf16[2,512,2048]{2,1,0:T(8,128)(2,1)}, bf16[2,512,2048]{2,1,0:T(8,128)(2,1)}, u32[]{:S(2)}, u32[]{:S(2)}) collective-permute-start(bf16[2,512,2048]{2,1,0:T(8,128)(2,1)} %get-tuple-element.43), channel_id=1, source_target_pairs={{0,4},{4,0},{1,5},{5,1},{2,6},{6,2},{3,7},{7,3}} | collective-permute-start | bytes 12582920 | tf_op jit(solution)/shard_map/ppermute | solution.py:256
  1087.9 313.6 %collective-permute-start.1 = (bf16[2,512,2048]{2,1,0:T(8,128)(2,1)}, bf16[2,512,2048]{2,1,0:T(8,128)(2,1)}, u32[]{:S(2)}, u32[]{:S(2)}) collective-permute-start(bf16[2,512,2048]{2,1,0:T(8,128)(2,1)} %get-tuple-element.41), channel_id=1, source_target_pairs={{0,4},{4,0},{1,5},{5,1},{2,6},{6,2},{3,7},{7,3}} | collective-permute-start | bytes 12582920 | tf_op jit(solution)/shard_map/ppermute | solution.py:256
  1089.8 34.0 %slice-start = ((s8[33554432]{0:T(1024)(128)(4,1)}), s8[4194304]{0:T(1024)(128)(4,1)S(1)}, s32[]{:S(2)}) async-start(s8[33554432]{0:T(1024)(128)(4,1)} %bitcast.146), calls=%async_computation.6 | async-start | bytes 8388608
  1089.9 34.0 %slice-start.1 = ((s8[33554432]{0:T(1024)(128)(4,1)}), s8[4194304]{0:T(1024)(128)(4,1)S(1)}, s32[]{:S(2)}) async-start(s8[33554432]{0:T(1024)(128)(4,1)} %bitcast.146), calls=%async_computation.7 | async-start | bytes 8388608
  1089.9 34.0 %slice-start.2 = ((s8[33554432]{0:T(1024)(128)(4,1)}), s8[4194304]{0:T(1024)(128)(4,1)S(1)}, s32[]{:S(2)}) async-start(s8[33554432]{0:T(1024)(128)(4,1)} %bitcast.146), calls=%async_computation.8 | async-start | bytes 8388608
  1089.9 34.0 %slice-start.3 = ((s8[33554432]{0:T(1024)(128)(4,1)}), s8[4194304]{0:T(1024)(128)(4,1)S(1)}, s32[]{:S(2)}) async-start(s8[33554432]{0:T(1024)(128)(4,1)} %bitcast.146), calls=%async_computation.9 | async-start | bytes 8388608
  1106.8 17.0 %slice-start.4 = ((s8[33554432]{0:T(1024)(128)(4,1)}), s8[4194304]{0:T(1024)(128)(4,1)S(1)}, s32[]{:S(2)}) async-start(s8[33554432]{0:T(1024)(128)(4,1)} %bitcast.146), calls=%async_computation.10 | async-start | bytes 8388608
  1106.8 17.0 %slice-start.5 = ((s8[33554432]{0:T(1024)(128)(4,1)}), s8[4194304]{0:T(1024)(128)(4,1)S(1)}, s32[]{:S(2)}) async-start(s8[33554432]{0:T(1024)(128)(4,1)} %bitcast.146), calls=%async_computation.11 | async-start | bytes 8388608
  1106.8 17.0 %slice-start.6 = ((s8[33554432]{0:T(1024)(128)(4,1)}), s8[4194304]{0:T(1024)(128)(4,1)S(1)}, s32[]{:S(2)}) async-start(s8[33554432]{0:T(1024)(128)(4,1)} %bitcast.146), calls=%async_computation.12 | async-start | bytes 8388608
  1106.8 17.0 %slice-start.7 = ((s8[33554432]{0:T(1024)(128)(4,1)}), s8[4194304]{0:T(1024)(128)(4,1)S(1)}, s32[]{:S(2)}) async-start(s8[33554432]{0:T(1024)(128)(4,1)} %bitcast.146), calls=%async_computation.13 | async-start | bytes 8388608
  1130.4 284.4 %copy-start.1 = (bf16[2048,768]{1,0:T(8,128)(2,1)S(1)}, bf16[2048,768]{1,0:T(8,128)(2,1)}, u32[]{:S(2)}) copy-start(bf16[2048,768]{1,0:T(8,128)(2,1)} %param.14) | copy-start | bytes 9437188
Sparse Core Ops, SparseCore 0:
  13.3 53.1 all-gather.6
  68.3 48.6 all-gather.10
  119.4 87.4 all-gather.8
  208.6 155.0 all-gather.12
  365.4 155.0 all-gather.14
  522.2 155.0 all-gather.16
